TPU v7x, 32 devices: a whole 2x2x4 slice. The times are simulated.
32 devices in a mesh: gx: 4 (over y, core), gy: 4 (over z), gz: 2 (over x).
Axes of the slice: x: 2, y: 2, z: 4, core: 2. Of those that a mesh axis runs over, the one named last changes fastest.
Arguments:
- face_blocks: float32 [4, 4, 2, 6, 16384], P('gx', 'gy', 'gz'), may hold values from -6 to 6
- owner_rank: int32 [4, 4, 2, 6, 1], P('gx', 'gy', 'gz'), may hold values from 0 to 3; in each aligned block of 6 rows (0 to 5, 6 to 11, ..., all dimensions but the last counted through in order) at most 2 rows name the same one
- owner_tile: int32 [4, 4, 2, 6], P('gx', 'gy', 'gz'), may hold values from 0 to 31
- live_count: int32 [4, 4, 2], P('gx', 'gy', 'gz'), may hold values from 1 to 6, as said below
- right_side: float32 [64, 256, 256], P('gx', 'gy', 'gz'), may hold values from -8 to 8
- diagonal: float32 [64, 256, 256], P('gx', 'gy', 'gz'), may hold values from 0.05 to 1
Outputs:
- solution_field: float32 [64, 256, 256], P('gx', 'gy', 'gz')
- residual: float32 [64, 256, 256], P('gx', 'gy', 'gz')
Inputs may be any that keep to these rules, and one draw needn't show every extreme that they name: `owner_rank`: on one device no owner is named by more than 2 of the 6 slots, live or not; some owner is named exactly 2 times on some devices. `live_count`: some device has all 6 slots live in every draw.
All inputs are finite; a program needn't handle non-finite values.
Results may differ from a plain program's by a relative error of at most 0.00012.
Values sent between devices are 32-bit elements; how exact they have to be, the bound alone decides.
A program may use at most 64 MiB of HBM per device.

v0:
```python
import functools
import math

import jax
import jax.numpy as jnp
from jax import lax
from jax.experimental import pallas as pl
from jax.experimental.pallas import tpu as pltpu
from jax.sharding import PartitionSpec as P

CAP = 2
AXES = ("gx", "gy", "gz")
MESH = pl.DeviceIdType.MESH
F32 = jnp.float32


def offsets_of(sizes, axes):
    found = [()]
    for axis in axes:
        found = [done + (step,) for done in found for step in range(sizes[axis])]
    return [dict(zip(axes, steps)) for steps in found if any(steps)]


def stages_of(sizes):
    stages = []
    for axis in ("gx", "gz", "gy"):
        if stages and math.prod(sizes[a] for a in stages[-1] + [axis]) <= 8:
            stages[-1].append(axis)
        else:
            stages.append([axis])
    return stages


def kernel(
    sizes, stages,
    rank_ref, tile_ref, live_hbm, face_hbm, right_hbm, diag_hbm,
    load_hbm, p_hbm, q_hbm, coef_ref,
    live_ref, face_v, load_v, diag_v, p_v, q_v, sums_v, send_v, recv_v, turned_v,
    hx_v, ysend_v, hy_v, zsend_v, hz_v, part_v, gath_v,
    in_sem, out_sem, a2a_send, a2a_recv, halo_send, halo_recv, red_send, red_recv,
):
    cx, cy, cz = load_v.shape
    blocks = face_v.shape[0]
    group = sizes["gx"]
    at = {axis: lax.axis_index(axis) for axis in AXES}

    def near(axis, side):
        return at[axis] > 0 if side == 0 else at[axis] < sizes[axis] - 1

    def beside(offset):
        return {a: lax.rem(at[a] + s, sizes[a]) for a, s in offset.items() if s}

    loads = [
        pltpu.make_async_copy(face_hbm, face_v, in_sem.at[0]),
        pltpu.make_async_copy(right_hbm, load_v, in_sem.at[1]),
        pltpu.make_async_copy(diag_hbm, diag_v, in_sem.at[2]),
        pltpu.make_async_copy(live_hbm, live_ref, in_sem.at[3]),
    ]
    for copy in loads:
        copy.start()

    for number, (axis, halo) in enumerate((("gx", hx_v), ("gy", hy_v), ("gz", hz_v))):
        for side in range(2):
            @pl.when(at[axis] == (0 if side == 0 else sizes[axis] - 1))
            def _():
                for turn in range(2):
                    halo[turn, side] = jnp.zeros(halo.shape[2:], F32)

    peers = {}
    for group_axes in [["gx"], ["gy"], ["gz"]] + stages:
        for offset in offsets_of(sizes, group_axes):
            peers[tuple(offset.get(a, 0) for a in AXES)] = offset
    barrier = pltpu.get_barrier_semaphore()
    for offset in peers.values():
        pl.semaphore_signal(barrier, inc=1, device_id=beside(offset), device_id_type=MESH)

    lane = lax.broadcasted_iota(jnp.int32, (cy, cz), 1)
    lane8 = lax.broadcasted_iota(jnp.int32, (8, cz), 1)
    row = lax.broadcasted_iota(jnp.int32, (cy, cz), 0)
    right_half = lane >= cz // 2

    loads[0].wait()
    loads[3].wait()
    pair = (
        lax.broadcasted_iota(jnp.int32, (cz, cz), 0) // 2
        == lax.broadcasted_iota(jnp.int32, (cz, cz), 1) % (cz // 2)
    )
    pair = jnp.where(pair, 0.25, 0.0).astype(jnp.bfloat16)
    for b in range(blocks):
        sums_v[b * cy:(b + 1) * cy] = (
            face_v[b, pl.ds(0, cy, stride=2), :] + face_v[b, pl.ds(1, cy, stride=2), :]
        )
    whole = sums_v[...]
    high = whole.astype(jnp.bfloat16)
    rest = whole - high.astype(F32)
    middle = rest.astype(jnp.bfloat16)
    low = (rest - middle.astype(F32)).astype(jnp.bfloat16)
    sums_v[...] = (
        jnp.dot(low, pair, preferred_element_type=F32)
        + jnp.dot(middle, pair, preferred_element_type=F32)
    ) + jnp.dot(high, pair, preferred_element_type=F32)

    target = [rank_ref[b] for b in range(blocks)]
    alive = [live_ref[0, 0, 0] > b for b in range(blocks)]
    position = []
    for b in range(blocks):
        count = jnp.int32(0)
        for before in range(b):
            count = count + jnp.where((target[before] == target[b]) & alive[before], 1, 0)
        position.append(count)
    for k in range(group):
        dest = lax.rem(at["gx"] + k, group)
        total = jnp.zeros((cy, cz), F32)
        tags = jnp.full((8, cz), -1.0, F32)
        for b in range(blocks):
            code = jnp.where(alive[b] & (target[b] == dest), position[b], CAP)
            left, right = jnp.where(code == 0, 1.0, 0.0), jnp.where(code == 1, 1.0, 0.0)
            weight = jnp.where(lane8 < cz // 2, left, right)
            tag = tile_ref[b].astype(F32)
            tags = jnp.where(weight > 0.5, tag, tags)
            values = sums_v[b * cy:(b + 1) * cy]
            total = total + values * jnp.where(right_half, right, left)
        (recv_v if k == 0 else send_v)[k, :cy] = total
        (recv_v if k == 0 else send_v)[k, cy:] = tags

    pl.semaphore_wait(barrier, len(peers))
    exchanges = []
    for k in range(1, group):
        copy = pltpu.make_async_remote_copy(
            src_ref=send_v.at[k], dst_ref=recv_v.at[k],
            send_sem=a2a_send.at[k], recv_sem=a2a_recv.at[k],
            device_id=beside({"gx": k}), device_id_type=MESH,
        )
        copy.start()
        exchanges.append(copy)
    loads[1].wait()
    loads[2].wait()
    for copy in exchanges:
        copy.wait_recv()

    for k in range(group):
        turned_v[k] = pltpu.roll(recv_v[k], cz // 2, axis=1)
    want = [(2 * x + jnp.where(lane8 >= cz // 2, 1, 0)).astype(F32)[:1] for x in range(cx)]
    order = [0, cx - 1] + list(range(1, cx - 1))

    def halo_copy(turn, axis, side, src):
        number, halo = AXES.index(axis), (hx_v, hy_v, hz_v)[AXES.index(axis)]
        step = sizes[axis] - 1 if side == 0 else 1
        return pltpu.make_async_remote_copy(
            src_ref=src, dst_ref=halo.at[turn, 1 - side],
            send_sem=halo_send.at[turn, 2 * number + side],
            recv_sem=halo_recv.at[turn, 2 * number + 1 - side],
            device_id={axis: lax.rem(at[axis] + step, sizes[axis])}, device_id_type=MESH,
        )

    def faces(turn, field, axis):
        if axis == "gx":
            return field.at[0], field.at[cx - 1]
        if axis == "gy":
            return ysend_v.at[turn, 0], ysend_v.at[turn, 1]
        return zsend_v.at[turn], zsend_v.at[turn]

    def send(turn, field, axis):
        for side in range(2):
            @pl.when(near(axis, side))
            def _():
                halo_copy(turn, axis, side, faces(turn, field, axis)[side]).start()

    def receive(turn, field, axis):
        for side in range(2):
            @pl.when(near(axis, side))
            def _():
                halo_copy(turn, axis, 1 - side, faces(turn, field, axis)[1 - side]).wait_recv()

    def finish(turn, field, axis):
        for side in range(2):
            @pl.when(near(axis, side))
            def _():
                halo_copy(turn, axis, side, faces(turn, field, axis)[side]).wait_send()

    def pack(turn, x, plane, packed):
        ysend_v[turn, 0, x:x + 1] = plane[:1]
        ysend_v[turn, 1, x:x + 1] = plane[cy - 1:]
        turned = plane if x == 0 else pltpu.roll(plane, 2 * x, axis=1)
        return jnp.where(((lane + 1) % cz) // 2 == x, turned, packed)

    packed = jnp.zeros((cy, cz), F32)
    for x in order:
        plane = load_v[x]
        for k in range(group):
            values, tags = recv_v[k, :cy], recv_v[k, cy:cy + 1]
            plane = plane + jnp.where(tags == want[x], values, 0.0)
            plane = plane + jnp.where(
                turned_v[k, cy:cy + 1] == want[x], turned_v[k, :cy], 0.0
            )
        load_v[x] = plane
        packed = pack(0, x, plane, packed)
        if x == cx - 1:
            send(0, load_v, "gx")
    zsend_v[0] = packed
    send(0, load_v, "gz")
    send(0, load_v, "gy")

    stores = [
        pltpu.make_async_copy(load_v, load_hbm, out_sem.at[0]),
        pltpu.make_async_copy(p_v, p_hbm, out_sem.at[1]),
        pltpu.make_async_copy(q_v, q_hbm, out_sem.at[2]),
    ]
    stores[0].start()

    def inside(src, dst):
        for x in range(cx):
            plane = src[x]
            around = jnp.where(lane == 0, 0.0, pltpu.roll(plane, 1, axis=1))
            around = around + jnp.where(lane == cz - 1, 0.0, pltpu.roll(plane, cz - 1, axis=1))
            around = around + jnp.where(row == 0, 0.0, pltpu.roll(plane, 1, axis=0))
            around = around + jnp.where(row == cy - 1, 0.0, pltpu.roll(plane, cy - 1, axis=0))
            if x > 0:
                around = around + src[x - 1]
            if x < cx - 1:
                around = around + src[x + 1]
            dst[x] = diag_v[x] * plane - around

    def fold(acc, values):
        for part in range(cy // 8):
            acc = acc + values[8 * part:8 * part + 8]
        return acc

    def border(turn, src, dst, sink):
        for axis in ("gx", "gz", "gy"):
            receive(turn, src, axis)
        ahead, behind = hz_v[turn, 1], pltpu.roll(hz_v[turn, 0], 2, axis=1)
        merged = jnp.where(lane % 2 == 0, ahead, behind)
        for x in order:
            edge = pltpu.roll(merged, cz - 2 * x - 1, axis=1)
            plane = dst[x] - jnp.where((lane == 0) | (lane == cz - 1), edge, 0.0)
            plane = plane - jnp.where(row == 0, hy_v[turn, 0, x:x + 1], 0.0)
            plane = plane - jnp.where(row == cy - 1, hy_v[turn, 1, x:x + 1], 0.0)
            if x == 0:
                plane = plane - hx_v[turn, 0]
            if x == cx - 1:
                plane = plane - hx_v[turn, 1]
            dst[x] = plane
            sink(x, plane)

    inside(load_v, p_v)
    state = {"packed": jnp.zeros((cy, cz), F32)}

    def first(x, plane):
        state["packed"] = pack(1, x, plane, state["packed"])
        if x == cx - 1:
            send(1, p_v, "gx")

    border(0, load_v, p_v, first)
    zsend_v[1] = state["packed"]
    send(1, p_v, "gz")
    send(1, p_v, "gy")
    stores[1].start()
    inside(p_v, q_v)
    acc = [jnp.zeros((8, cz), F32) for _ in range(4)]
    for x in range(cx):
        load, p = load_v[x], p_v[x]
        acc[0], acc[1], acc[2] = fold(acc[0], load * load), fold(acc[1], load * p), fold(acc[2], p * p)

    def second(x, plane):
        acc[3] = fold(acc[3], plane * p_v[x])

    border(1, p_v, q_v, second)
    stores[2].start()

    row8 = lax.broadcasted_iota(jnp.int32, (8, cz), 0)
    mine = jnp.zeros((8, cz), F32)
    for number in range(4):
        mine = jnp.where(row8 == number, jnp.sum(acc[number], axis=0, keepdims=True), mine)
    slot = 0
    waiting = []
    for number, axes in enumerate(stages):
        part_v[number] = mine
        copies = []
        for offset in offsets_of(sizes, axes):
            copy = pltpu.make_async_remote_copy(
                src_ref=part_v.at[number], dst_ref=gath_v.at[slot],
                send_sem=red_send.at[slot], recv_sem=red_recv.at[slot],
                device_id=beside(offset), device_id_type=MESH,
            )
            copy.start()
            copies.append((slot, copy))
            slot += 1
        for at_slot, copy in copies:
            copy.wait_recv()
            mine = mine + gath_v[at_slot]
        waiting += [copy for _, copy in copies]

    sums = jnp.sum(mine, axis=1, keepdims=True)
    s0, s1, s2, s3 = (sums[n:n + 1] for n in range(4))
    step = 6.0 * s0 + s1
    a = s0 / step
    c = s1 / step
    norm = c * c * s0 - 2.0 * a * c * s1 + a * a * s2
    e = c + norm / s0
    curve = 6.0 * (e * e * s0 - 2.0 * e * a * s1 + a * a * s2) + (
        e * e * s1 - 2.0 * e * a * s2 + a * a * s3
    )
    b = norm / curve
    x_load, x_p = a + b * e, b * a
    r_load, r_p, r_q = c - 6.0 * b * e, a + b * (e - 6.0 * a), b * a
    for number, value in enumerate((x_load, x_p, r_load, r_p, r_q)):
        coef_ref[number:number + 1] = jnp.broadcast_to(value, (1, cz))
    for copy in stores:
        copy.wait()
    for copy in exchanges + waiting:
        copy.wait_send()
    for turn, field in ((0, load_v), (1, p_v)):
        for axis in AXES:
            finish(turn, field, axis)


def combine(load_ref, p_ref, q_ref, coef_ref, x_ref, r_ref):
    x_load, x_p, r_load, r_p, r_q = (coef_ref[n:n + 1] for n in range(5))
    for x in range(load_ref.shape[0]):
        load, p = load_ref[x], p_ref[x]
        x_ref[x] = x_load * load - x_p * p
        r_ref[x] = r_load * load - r_p * p + r_q * q_ref[x]


def combined(load, p, q, coef):
    cx, cy, cz = load.shape
    parts = 2 if cx % 2 == 0 else 1
    piece = pl.BlockSpec((cx // parts, cy, cz), lambda i: (i, 0, 0))
    box = jax.ShapeDtypeStruct((cx, cy, cz), F32)
    return pl.pallas_call(
        combine,
        grid=(parts,),
        out_shape=(box, box),
        in_specs=[piece] * 3 + [pl.BlockSpec((8, cz), lambda i: (0, 0))],
        out_specs=(piece, piece),
    )(load, p, q, coef)


def per_device(sizes, face_blocks, owner_rank, owner_tile, live_count, right_side, diagonal):
    blocks = face_blocks.shape[3]
    cx, cy, cz = right_side.shape
    group = sizes["gx"]
    stages = stages_of(sizes)
    slots = sum(len(offsets_of(sizes, axes)) for axes in stages)
    smem, vmem, anywhere = (
        pl.BlockSpec(memory_space=space) for space in (pltpu.SMEM, pltpu.VMEM, pl.ANY)
    )
    box = jax.ShapeDtypeStruct((cx, cy, cz), F32)
    load, p, q, coef = pl.pallas_call(
        functools.partial(kernel, sizes, stages),
        out_shape=(box, box, box, jax.ShapeDtypeStruct((8, cz), F32)),
        in_specs=[smem] * 2 + [anywhere] * 4,
        out_specs=(anywhere, anywhere, anywhere, vmem),
        scratch_shapes=[
            pltpu.SMEM(live_count.shape, jnp.int32),
            pltpu.VMEM((blocks, 2 * cy, cz), F32),
            pltpu.VMEM((cx, cy, cz), F32),
            pltpu.VMEM((cx, cy, cz), F32),
            pltpu.VMEM((cx, cy, cz), F32),
            pltpu.VMEM((cx, cy, cz), F32),
            pltpu.VMEM((blocks * cy, cz), F32),
            pltpu.VMEM((group, cy + 8, cz), F32),
            pltpu.VMEM((group, cy + 8, cz), F32),
            pltpu.VMEM((group, cy + 8, cz), F32),
            pltpu.VMEM((2, 2, cy, cz), F32),
            pltpu.VMEM((2, 2, cx, cz), F32),
            pltpu.VMEM((2, 2, cx, cz), F32),
            pltpu.VMEM((2, cy, cz), F32),
            pltpu.VMEM((2, 2, cy, cz), F32),
            pltpu.VMEM((len(stages), 8, cz), F32),
            pltpu.VMEM((slots, 8, cz), F32),
            pltpu.SemaphoreType.DMA((4,)),
            pltpu.SemaphoreType.DMA((3,)),
            pltpu.SemaphoreType.DMA((group,)),
            pltpu.SemaphoreType.DMA((group,)),
            pltpu.SemaphoreType.DMA((2, 6)),
            pltpu.SemaphoreType.DMA((2, 6)),
            pltpu.SemaphoreType.DMA((slots,)),
            pltpu.SemaphoreType.DMA((slots,)),
        ],
        compiler_params=pltpu.CompilerParams(collective_id=0, has_side_effects=True),
    )(
        owner_rank.reshape(blocks), owner_tile.reshape(blocks), live_count,
        face_blocks.reshape(blocks, 2 * cy, cz), right_side, diagonal,
    )
    return combined(load, p, q, coef)


def solution(mesh):
    sizes = dict(mesh.shape)
    return jax.shard_map(
        functools.partial(per_device, sizes),
        mesh=mesh,
        in_specs=(
            P("gx", "gy", "gz", None, None),
            P("gx", "gy", "gz", None, None),
            P("gx", "gy", "gz", None),
            P("gx", "gy", "gz"),
            P("gx", "gy", "gz"),
            P("gx", "gy", "gz"),
        ),
        out_specs=(P("gx", "gy", "gz"), P("gx", "gy", "gz")),
        check_vma=False,
    )
```

profile of v0, /device:TPU:0, one launch (start us, length us, event | category | flops | bytes accessed | tf_op | source)
XLA Modules:
  0.0 28.1 jit_solution(857470893454359921)
XLA Ops:
  1.3 24.6 %shard_map.77 = (f32[16,64,128]{2,1,0:T(8,128)}, f32[16,64,128]{2,1,0:T(8,128)}, f32[16,64,128]{2,1,0:T(8,128)}, f32[8,128]{1,0:T(8,128)}) custom-call(s32[6]{0:T(128)} %bitcast.4, s32[6]{0:T(128)} %bitcast.5, s32[1,1,1]{2,1,0:T(1,128)S(6)} %copy.8.live_hbm, f32[6,128,128]{2,1,0:T(8,128)} %bitcast.3, f32[16,64,128]{2,1,0:T(8,128)} %right_hbm.1, ...), custom_call_target="tpu_custom_call" | custom-call | tf_op jit(solution)/shard_map/pallas_call | solution.py:350
  25.9 2.2 %shard_map.78 = (f32[16,64,128]{2,1,0:T(8,128)}, f32[16,64,128]{2,1,0:T(8,128)}) custom-call(f32[16,64,128]{2,1,0:T(8,128)} %get-tuple-element.6.load_ref, f32[16,64,128]{2,1,0:T(8,128)} %get-tuple-element.7.p_ref, f32[16,64,128]{2,1,0:T(8,128)} %get-tuple-element.8.q_ref, f32[8,128]{1,0:T(8,128)} %get-tuple-element.9.coef_ref), custom_call_target="tpu_custom_call" | custom-call | tf_op jit(solution)/shard_map/pallas_call | solution.py:331
where the time goes:
time: 28.3 us; the launch traced here: 28.1 us
  Pallas kernels  26.8 us (95%)
  between operations  1.28 us (5%)
    pallas_call x1, Pallas kernels, per_device(): pl.pallas_call(functools.partial(kernel, sizes, stages), out_shape=(box,...  24.6 us
    pallas_call x1, Pallas kernels, combined(): pl.pallas_call(combine, grid=(parts,), out_shape=(box, box), in_specs=[pi...  2.23 us

commit v1 on v0

--- a/solution.py
+++ b/solution.py
@@ -33,11 +33,11 @@
 
 def kernel(
     sizes, stages,
-    rank_ref, tile_ref, live_hbm, face_hbm, right_hbm, diag_hbm,
-    load_hbm, p_hbm, q_hbm, coef_ref,
-    live_ref, face_v, load_v, diag_v, p_v, q_v, sums_v, send_v, recv_v, turned_v,
+    rank_hbm, tile_hbm, live_hbm, face_hbm, right_hbm, diag_hbm,
+    load_v, p_v, q_v, coef_ref,
+    rank_ref, tile_ref, live_ref, face_v, diag_v, sums_v, send_v, recv_v, turned_v,
     hx_v, ysend_v, hy_v, zsend_v, hz_v, part_v, gath_v,
-    in_sem, out_sem, a2a_send, a2a_recv, halo_send, halo_recv, red_send, red_recv,
+    in_sem, a2a_send, a2a_recv, halo_send, halo_recv, red_send, red_recv,
 ):
     cx, cy, cz = load_v.shape
     blocks = face_v.shape[0]
@@ -55,6 +55,8 @@
         pltpu.make_async_copy(right_hbm, load_v, in_sem.at[1]),
         pltpu.make_async_copy(diag_hbm, diag_v, in_sem.at[2]),
         pltpu.make_async_copy(live_hbm, live_ref, in_sem.at[3]),
+        pltpu.make_async_copy(rank_hbm, rank_ref, in_sem.at[4]),
+        pltpu.make_async_copy(tile_hbm, tile_ref, in_sem.at[5]),
     ]
     for copy in loads:
         copy.start()
@@ -80,7 +82,8 @@
     right_half = lane >= cz // 2
 
     loads[0].wait()
-    loads[3].wait()
+    for copy in loads[3:]:
+        copy.wait()
     pair = (
         lax.broadcasted_iota(jnp.int32, (cz, cz), 0) // 2
         == lax.broadcasted_iota(jnp.int32, (cz, cz), 1) % (cz // 2)
@@ -201,13 +204,6 @@
     send(0, load_v, "gz")
     send(0, load_v, "gy")
 
-    stores = [
-        pltpu.make_async_copy(load_v, load_hbm, out_sem.at[0]),
-        pltpu.make_async_copy(p_v, p_hbm, out_sem.at[1]),
-        pltpu.make_async_copy(q_v, q_hbm, out_sem.at[2]),
-    ]
-    stores[0].start()
-
     def inside(src, dst):
         for x in range(cx):
             plane = src[x]
@@ -255,7 +251,6 @@
     zsend_v[1] = state["packed"]
     send(1, p_v, "gz")
     send(1, p_v, "gy")
-    stores[1].start()
     inside(p_v, q_v)
     acc = [jnp.zeros((8, cz), F32) for _ in range(4)]
     for x in range(cx):
@@ -266,7 +261,6 @@
         acc[3] = fold(acc[3], plane * p_v[x])
 
     border(1, p_v, q_v, second)
-    stores[2].start()
 
     row8 = lax.broadcasted_iota(jnp.int32, (8, cz), 0)
     mine = jnp.zeros((8, cz), F32)
@@ -306,8 +300,6 @@
     r_load, r_p, r_q = c - 6.0 * b * e, a + b * (e - 6.0 * a), b * a
     for number, value in enumerate((x_load, x_p, r_load, r_p, r_q)):
         coef_ref[number:number + 1] = jnp.broadcast_to(value, (1, cz))
-    for copy in stores:
-        copy.wait()
     for copy in exchanges + waiting:
         copy.wait_send()
     for turn, field in ((0, load_v), (1, p_v)):
@@ -315,26 +307,37 @@
             finish(turn, field, axis)
 
 
-def combine(load_ref, p_ref, q_ref, coef_ref, x_ref, r_ref):
+def combine(load_ref, p_ref, q_ref, coef_ref, x_hbm, r_hbm, x_v, r_v, sem):
+    cx = load_ref.shape[0]
     x_load, x_p, r_load, r_p, r_q = (coef_ref[n:n + 1] for n in range(5))
-    for x in range(load_ref.shape[0]):
-        load, p = load_ref[x], p_ref[x]
-        x_ref[x] = x_load * load - x_p * p
-        r_ref[x] = r_load * load - r_p * p + r_q * q_ref[x]
+    pieces = sem.shape[1]
+    copies = []
+    for piece in range(pieces):
+        first, last = cx * piece // pieces, cx * (piece + 1) // pieces
+        for x in range(first, last):
+            load, p = load_ref[x], p_ref[x]
+            x_v[x] = x_load * load - x_p * p
+            r_v[x] = r_load * load - r_p * p + r_q * q_ref[x]
+        span = pl.ds(first, last - first)
+        for number, (src, dst) in enumerate(((x_v, x_hbm), (r_v, r_hbm))):
+            copy = pltpu.make_async_copy(src.at[span], dst.at[span], sem.at[number, piece])
+            copy.start()
+            copies.append(copy)
+    for copy in copies:
+        copy.wait()
 
 
 def combined(load, p, q, coef):
     cx, cy, cz = load.shape
-    parts = 2 if cx % 2 == 0 else 1
-    piece = pl.BlockSpec((cx // parts, cy, cz), lambda i: (i, 0, 0))
     box = jax.ShapeDtypeStruct((cx, cy, cz), F32)
+    vmem, hbm = (pl.BlockSpec(memory_space=space) for space in (pltpu.VMEM, pltpu.HBM))
     return pl.pallas_call(
         combine,
-        grid=(parts,),
         out_shape=(box, box),
-        in_specs=[piece] * 3 + [pl.BlockSpec((8, cz), lambda i: (0, 0))],
-        out_specs=(piece, piece),
-    )(load, p, q, coef)
+        in_specs=[vmem] * 4,
+        out_specs=(hbm, hbm),
+        scratch_shapes=[pltpu.VMEM((cx, cy, cz), F32)] * 2 + [pltpu.SemaphoreType.DMA((2, 4))],
+    )(*(pltpu.with_memory_space_constraint(a, pltpu.VMEM) for a in (load, p, q, coef)))
 
 
 def per_device(sizes, face_blocks, owner_rank, owner_tile, live_count, right_side, diagonal):
@@ -343,21 +346,18 @@
     group = sizes["gx"]
     stages = stages_of(sizes)
     slots = sum(len(offsets_of(sizes, axes)) for axes in stages)
-    smem, vmem, anywhere = (
-        pl.BlockSpec(memory_space=space) for space in (pltpu.SMEM, pltpu.VMEM, pl.ANY)
-    )
-    box = jax.ShapeDtypeStruct((cx, cy, cz), F32)
+    vmem, hbm = (pl.BlockSpec(memory_space=space) for space in (pltpu.VMEM, pltpu.HBM))
+    box = pltpu.VMEM((cx, cy, cz), F32)
     load, p, q, coef = pl.pallas_call(
         functools.partial(kernel, sizes, stages),
-        out_shape=(box, box, box, jax.ShapeDtypeStruct((8, cz), F32)),
-        in_specs=[smem] * 2 + [anywhere] * 4,
-        out_specs=(anywhere, anywhere, anywhere, vmem),
+        out_shape=(box, box, box, pltpu.VMEM((8, cz), F32)),
+        in_specs=[hbm] * 6,
+        out_specs=(vmem, vmem, vmem, vmem),
         scratch_shapes=[
+            pltpu.SMEM((blocks,), jnp.int32),
+            pltpu.SMEM((blocks,), jnp.int32),
             pltpu.SMEM(live_count.shape, jnp.int32),
             pltpu.VMEM((blocks, 2 * cy, cz), F32),
-            pltpu.VMEM((cx, cy, cz), F32),
-            pltpu.VMEM((cx, cy, cz), F32),
-            pltpu.VMEM((cx, cy, cz), F32),
             pltpu.VMEM((cx, cy, cz), F32),
             pltpu.VMEM((blocks * cy, cz), F32),
             pltpu.VMEM((group, cy + 8, cz), F32),
@@ -370,8 +370,7 @@
             pltpu.VMEM((2, 2, cy, cz), F32),
             pltpu.VMEM((len(stages), 8, cz), F32),
             pltpu.VMEM((slots, 8, cz), F32),
-            pltpu.SemaphoreType.DMA((4,)),
-            pltpu.SemaphoreType.DMA((3,)),
+            pltpu.SemaphoreType.DMA((6,)),
             pltpu.SemaphoreType.DMA((group,)),
             pltpu.SemaphoreType.DMA((group,)),
             pltpu.SemaphoreType.DMA((2, 6)),
@@ -381,7 +380,8 @@
         ],
         compiler_params=pltpu.CompilerParams(collective_id=0, has_side_effects=True),
     )(
-        owner_rank.reshape(blocks), owner_tile.reshape(blocks), live_count,
+        owner_rank.reshape(blocks), owner_tile.reshape(blocks),
+        live_count,
         face_blocks.reshape(blocks, 2 * cy, cz), right_side, diagonal,
     )
     return combined(load, p, q, coef)

time: 28.3 us -> 25.8 us (0.912)
  Pallas kernels: 26.8 us -> 24.4 us
    pallas_call x1, Pallas kernels: 24.6 us -> 23.3 us  [per_device(): pl.pallas_call(functools.partial(kernel, sizes, stages), out_shape=(box,...]
    pallas_call x1, Pallas kernels: 2.23 us -> 1.05 us  [combined(): pl.pallas_call(combine, out_shape=(box, box), in_specs=[vmem] * 4, out_sp...]
where the time goes in v1:
time: 25.8 us; the launch traced here: 25.6 us
  Pallas kernels  24.4 us (95%)
  between operations  1.28 us (5%)
    pallas_call x1, Pallas kernels, per_device(): pl.pallas_call(functools.partial(kernel, sizes, stages), out_shape=(box,...  23.3 us
    pallas_call x1, Pallas kernels, combined(): pl.pallas_call(combine, out_shape=(box, box), in_specs=[vmem] * 4, out_sp...  1.05 us

profile of v1, /device:TPU:0, one launch (start us, length us, event | category | flops | bytes accessed | tf_op | source)
XLA Modules:
  0.0 25.6 jit_solution(3462999664744655639)
XLA Ops:
  1.3 23.3 %shard_map.77 = (f32[16,64,128]{2,1,0:T(8,128)S(1)}, f32[16,64,128]{2,1,0:T(8,128)S(1)}, f32[16,64,128]{2,1,0:T(8,128)S(1)}, f32[8,128]{1,0:T(8,128)S(1)}) custom-call(s32[6]{0:T(128)} %bitcast.4, s32[6]{0:T(128)} %bitcast.5, s32[1,1,1]{2,1,0:T(1,128)S(6)} %copy.8.live_hbm, f32[6,128,128]{2,1,0:T(8,128)} %bitcast.3, f32[16,64,128]{2,1,0:T(8,128)} %right_hbm.1, ...), custom_call_target="tpu_custom_call" | custom-call | tf_op jit(solution)/shard_map/pallas_call | solution.py:351
  24.6 1.0 %shard_map.78 = (f32[16,64,128]{2,1,0:T(8,128)}, f32[16,64,128]{2,1,0:T(8,128)}) custom-call(f32[16,64,128]{2,1,0:T(8,128)S(1)} %get-tuple-element.6.load_ref, f32[16,64,128]{2,1,0:T(8,128)S(1)} %get-tuple-element.7.p_ref, f32[16,64,128]{2,1,0:T(8,128)S(1)} %get-tuple-element.8.q_ref, f32[8,128]{1,0:T(8,128)S(1)} %get-tuple-element.9.coef_ref), custom_call_target="tpu_custom_call" | custom-call | tf_op jit(solution)/shard_map/pallas_call | solution.py:334

commit v2 on v1

--- a/solution.py
+++ b/solution.py
@@ -24,20 +24,28 @@
 def stages_of(sizes):
     stages = []
     for axis in ("gx", "gz", "gy"):
-        if stages and math.prod(sizes[a] for a in stages[-1] + [axis]) <= 8:
+        if stages and math.prod(sizes[a] for a in stages[-1] + [axis]) <= 32:
             stages[-1].append(axis)
         else:
             stages.append([axis])
     return stages
 
 
+def relays_of(sizes, stages):
+    reach = max(
+        sum(1 if axis == "gx" else sizes[axis] - 1 for axis in axes if sizes[axis] > 1)
+        for axes in stages
+    )
+    return max(1, reach - 2)
+
+
 def kernel(
-    sizes, stages,
+    sizes, stages, relays,
     rank_hbm, tile_hbm, live_hbm, face_hbm, right_hbm, diag_hbm,
     load_v, p_v, q_v, coef_ref,
-    rank_ref, tile_ref, live_ref, face_v, diag_v, sums_v, send_v, recv_v, turned_v,
+    rank_ref, tile_ref, live_ref, face_v, diag_v, sums_v, send_v, stag_v, recv_v, rtag_v, turned_v,
     hx_v, ysend_v, hy_v, zsend_v, hz_v, part_v, gath_v,
-    in_sem, a2a_send, a2a_recv, halo_send, halo_recv, red_send, red_recv,
+    in_sem, a2a_send, a2a_recv, relay_sem, halo_send, halo_recv, red_send, red_recv,
 ):
     cx, cy, cz = load_v.shape
     blocks = face_v.shape[0]
@@ -68,15 +76,29 @@
                 for turn in range(2):
                     halo[turn, side] = jnp.zeros(halo.shape[2:], F32)
 
-    peers = {}
-    for group_axes in [["gx"], ["gy"], ["gz"]] + stages:
-        for offset in offsets_of(sizes, group_axes):
-            peers[tuple(offset.get(a, 0) for a in AXES)] = offset
+    def greet(semaphore):
+        for k in range(1, group):
+            pl.semaphore_signal(
+                semaphore, inc=1, device_id=beside({"gx": k}), device_id_type=MESH
+            )
+        for axis in ("gy", "gz"):
+            for side in range(2):
+                @pl.when(near(axis, side))
+                def _():
+                    pl.semaphore_signal(
+                        semaphore, inc=1, device_id={axis: at[axis] + 2 * side - 1},
+                        device_id_type=MESH,
+                    )
+
+    greeted = jnp.int32(group - 1)
+    for axis in ("gy", "gz"):
+        for side in range(2):
+            greeted = greeted + jnp.where(near(axis, side), 1, 0)
     barrier = pltpu.get_barrier_semaphore()
-    for offset in peers.values():
-        pl.semaphore_signal(barrier, inc=1, device_id=beside(offset), device_id_type=MESH)
+    greet(barrier)
 
     lane = lax.broadcasted_iota(jnp.int32, (cy, cz), 1)
+    lane1 = lax.broadcasted_iota(jnp.int32, (1, cz), 1)
     lane8 = lax.broadcasted_iota(jnp.int32, (8, cz), 1)
     row = lax.broadcasted_iota(jnp.int32, (cy, cz), 0)
     right_half = lane >= cz // 2
@@ -114,28 +136,33 @@
     for k in range(group):
         dest = lax.rem(at["gx"] + k, group)
         total = jnp.zeros((cy, cz), F32)
-        tags = jnp.full((8, cz), -1.0, F32)
+        tags = jnp.full((1, cz), -1.0, F32)
         for b in range(blocks):
             code = jnp.where(alive[b] & (target[b] == dest), position[b], CAP)
             left, right = jnp.where(code == 0, 1.0, 0.0), jnp.where(code == 1, 1.0, 0.0)
-            weight = jnp.where(lane8 < cz // 2, left, right)
+            weight = jnp.where(lane1 < cz // 2, left, right)
             tag = tile_ref[b].astype(F32)
             tags = jnp.where(weight > 0.5, tag, tags)
             values = sums_v[b * cy:(b + 1) * cy]
             total = total + values * jnp.where(right_half, right, left)
-        (recv_v if k == 0 else send_v)[k, :cy] = total
-        (recv_v if k == 0 else send_v)[k, cy:] = tags
-
-    pl.semaphore_wait(barrier, len(peers))
+        (recv_v if k == 0 else send_v)[k] = total
+        (rtag_v if k == 0 else stag_v)[k] = tags
+
+    pl.semaphore_wait(barrier, greeted)
     exchanges = []
     for k in range(1, group):
-        copy = pltpu.make_async_remote_copy(
-            src_ref=send_v.at[k], dst_ref=recv_v.at[k],
-            send_sem=a2a_send.at[k], recv_sem=a2a_recv.at[k],
-            device_id=beside({"gx": k}), device_id_type=MESH,
-        )
-        copy.start()
-        exchanges.append(copy)
+        for number, (src, dst) in enumerate(((send_v, recv_v), (stag_v, rtag_v))):
+            copy = pltpu.make_async_remote_copy(
+                src_ref=src.at[k], dst_ref=dst.at[k],
+                send_sem=a2a_send.at[number, k], recv_sem=a2a_recv.at[number, k],
+                device_id=beside({"gx": k}), device_id_type=MESH,
+            )
+            copy.start()
+            exchanges.append(copy)
+    for relay in range(relays - 1):
+        greet(relay_sem.at[relay])
+        pl.semaphore_wait(relay_sem.at[relay], greeted)
+    greet(relay_sem.at[relays - 1])
     loads[1].wait()
     loads[2].wait()
     for copy in exchanges:
@@ -143,7 +170,11 @@
 
     for k in range(group):
         turned_v[k] = pltpu.roll(recv_v[k], cz // 2, axis=1)
-    want = [(2 * x + jnp.where(lane8 >= cz // 2, 1, 0)).astype(F32)[:1] for x in range(cx)]
+    tags_of = [rtag_v[k] for k in range(group)]
+    turned_tags = [
+        pltpu.roll(jnp.broadcast_to(tags, (8, cz)), cz // 2, axis=1)[:1] for tags in tags_of
+    ]
+    want = [(2 * x + jnp.where(lane1 >= cz // 2, 1, 0)).astype(F32) for x in range(cx)]
     order = [0, cx - 1] + list(range(1, cx - 1))
 
     def halo_copy(turn, axis, side, src):
@@ -191,11 +222,8 @@
     for x in order:
         plane = load_v[x]
         for k in range(group):
-            values, tags = recv_v[k, :cy], recv_v[k, cy:cy + 1]
-            plane = plane + jnp.where(tags == want[x], values, 0.0)
-            plane = plane + jnp.where(
-                turned_v[k, cy:cy + 1] == want[x], turned_v[k, :cy], 0.0
-            )
+            plane = plane + jnp.where(tags_of[k] == want[x], recv_v[k], 0.0)
+            plane = plane + jnp.where(turned_tags[k] == want[x], turned_v[k], 0.0)
         load_v[x] = plane
         packed = pack(0, x, plane, packed)
         if x == cx - 1:
@@ -239,6 +267,7 @@
             dst[x] = plane
             sink(x, plane)
 
+    pl.semaphore_wait(relay_sem.at[relays - 1], greeted)
     inside(load_v, p_v)
     state = {"packed": jnp.zeros((cy, cz), F32)}
 
@@ -266,6 +295,10 @@
     mine = jnp.zeros((8, cz), F32)
     for number in range(4):
         mine = jnp.where(row8 == number, jnp.sum(acc[number], axis=0, keepdims=True), mine)
+    mine = mine + pltpu.roll(mine, cz // 2, axis=1)
+    mine = mine + pltpu.roll(mine, cz // 4, axis=1)
+    own = row8 == lane8 // (cz // 4)
+    mine = jnp.sum(jnp.where(own, mine, 0.0), axis=0, keepdims=True)
     slot = 0
     waiting = []
     for number, axes in enumerate(stages):
@@ -285,7 +318,7 @@
             mine = mine + gath_v[at_slot]
         waiting += [copy for _, copy in copies]
 
-    sums = jnp.sum(mine, axis=1, keepdims=True)
+    sums = jnp.sum(jnp.where(own, mine, 0.0), axis=1, keepdims=True)
     s0, s1, s2, s3 = (sums[n:n + 1] for n in range(4))
     step = 6.0 * s0 + s1
     a = s0 / step
@@ -345,11 +378,12 @@
     cx, cy, cz = right_side.shape
     group = sizes["gx"]
     stages = stages_of(sizes)
+    relays = relays_of(sizes, stages)
     slots = sum(len(offsets_of(sizes, axes)) for axes in stages)
     vmem, hbm = (pl.BlockSpec(memory_space=space) for space in (pltpu.VMEM, pltpu.HBM))
     box = pltpu.VMEM((cx, cy, cz), F32)
     load, p, q, coef = pl.pallas_call(
-        functools.partial(kernel, sizes, stages),
+        functools.partial(kernel, sizes, stages, relays),
         out_shape=(box, box, box, pltpu.VMEM((8, cz), F32)),
         in_specs=[hbm] * 6,
         out_specs=(vmem, vmem, vmem, vmem),
@@ -360,19 +394,22 @@
             pltpu.VMEM((blocks, 2 * cy, cz), F32),
             pltpu.VMEM((cx, cy, cz), F32),
             pltpu.VMEM((blocks * cy, cz), F32),
-            pltpu.VMEM((group, cy + 8, cz), F32),
-            pltpu.VMEM((group, cy + 8, cz), F32),
-            pltpu.VMEM((group, cy + 8, cz), F32),
+            pltpu.VMEM((group, cy, cz), F32),
+            pltpu.VMEM((group, 1, cz), F32),
+            pltpu.VMEM((group, cy, cz), F32),
+            pltpu.VMEM((group, 1, cz), F32),
+            pltpu.VMEM((group, cy, cz), F32),
             pltpu.VMEM((2, 2, cy, cz), F32),
             pltpu.VMEM((2, 2, cx, cz), F32),
             pltpu.VMEM((2, 2, cx, cz), F32),
             pltpu.VMEM((2, cy, cz), F32),
             pltpu.VMEM((2, 2, cy, cz), F32),
-            pltpu.VMEM((len(stages), 8, cz), F32),
-            pltpu.VMEM((slots, 8, cz), F32),
+            pltpu.VMEM((len(stages), 1, cz), F32),
+            pltpu.VMEM((slots, 1, cz), F32),
             pltpu.SemaphoreType.DMA((6,)),
-            pltpu.SemaphoreType.DMA((group,)),
-            pltpu.SemaphoreType.DMA((group,)),
+            pltpu.SemaphoreType.DMA((2, group)),
+            pltpu.SemaphoreType.DMA((2, group)),
+            pltpu.SemaphoreType.REGULAR((relays,)),
             pltpu.SemaphoreType.DMA((2, 6)),
             pltpu.SemaphoreType.DMA((2, 6)),
             pltpu.SemaphoreType.DMA((slots,)),

time: 25.8 us -> 24.2 us (0.938)
  Pallas kernels: 24.4 us -> 22.7 us
    pallas_call x1, Pallas kernels: 23.3 us -> 21.7 us  [per_device(): pl.pallas_call(functools.partial(kernel, sizes, stages, relays), out_shap...]
where the time goes in v2:
time: 24.2 us; the launch traced here: 24 us
  Pallas kernels  22.7 us (94%)
  between operations  1.28 us (5%)
    pallas_call x1, Pallas kernels, per_device(): pl.pallas_call(functools.partial(kernel, sizes, stages, relays), out_shap...  21.7 us
    pallas_call x1, Pallas kernels, combined(): pl.pallas_call(combine, out_shape=(box, box), in_specs=[vmem] * 4, out_sp...  1.05 us

profile of v2, /device:TPU:0, one launch (start us, length us, event | category | flops | bytes accessed | tf_op | source)
XLA Modules:
  0.0 24.0 jit_solution(17000770816225513500)
XLA Ops:
  1.3 21.7 %shard_map.77 = (f32[16,64,128]{2,1,0:T(8,128)S(1)}, f32[16,64,128]{2,1,0:T(8,128)S(1)}, f32[16,64,128]{2,1,0:T(8,128)S(1)}, f32[8,128]{1,0:T(8,128)S(1)}) custom-call(s32[6]{0:T(128)} %bitcast.4, s32[6]{0:T(128)} %bitcast.5, s32[1,1,1]{2,1,0:T(1,128)S(6)} %copy.8.live_hbm, f32[6,128,128]{2,1,0:T(8,128)} %bitcast.3, f32[16,64,128]{2,1,0:T(8,128)} %right_hbm.1, ...), custom_call_target="tpu_custom_call" | custom-call | tf_op jit(solution)/shard_map/pallas_call | solution.py:385
  23.0 1.0 %shard_map.78 = (f32[16,64,128]{2,1,0:T(8,128)}, f32[16,64,128]{2,1,0:T(8,128)}) custom-call(f32[16,64,128]{2,1,0:T(8,128)S(1)} %get-tuple-element.6.load_ref, f32[16,64,128]{2,1,0:T(8,128)S(1)} %get-tuple-element.7.p_ref, f32[16,64,128]{2,1,0:T(8,128)S(1)} %get-tuple-element.8.q_ref, f32[8,128]{1,0:T(8,128)S(1)} %get-tuple-element.9.coef_ref), custom_call_target="tpu_custom_call" | custom-call | tf_op jit(solution)/shard_map/pallas_call | solution.py:367

commit v3 on v2

--- a/solution.py
+++ b/solution.py
@@ -43,13 +43,15 @@
     sizes, stages, relays,
     rank_hbm, tile_hbm, live_hbm, face_hbm, right_hbm, diag_hbm,
     load_v, p_v, q_v, coef_ref,
-    rank_ref, tile_ref, live_ref, face_v, diag_v, sums_v, send_v, stag_v, recv_v, rtag_v, turned_v,
-    hx_v, ysend_v, hy_v, zsend_v, hz_v, part_v, gath_v,
+    rank_ref, tile_ref, live_ref, face_v, diag_v, sums_v,
+    send_v, stag_v, recv_v, rtag_v, turned_v, rows_v, drows_v, cols_v,
+    hx_v, ysend_v, hy_v, zsend_v, hz_v, xy_v, hxy_v, yz_v, hyz_v, xz_v, hxz_v, part_v, gath_v,
     in_sem, a2a_send, a2a_recv, relay_sem, halo_send, halo_recv, red_send, red_recv,
 ):
     cx, cy, cz = load_v.shape
     blocks = face_v.shape[0]
     group = sizes["gx"]
+    folds = cy // zsend_v.shape[0]
     at = {axis: lax.axis_index(axis) for axis in AXES}
 
     def near(axis, side):
@@ -57,6 +59,12 @@
 
     def beside(offset):
         return {a: lax.rem(at[a] + s, sizes[a]) for a, s in offset.items() if s}
+
+    def near_all(sides):
+        found = near(*sides[0])
+        for axis, side in sides[1:]:
+            found = found & near(axis, side)
+        return found
 
     loads = [
         pltpu.make_async_copy(face_hbm, face_v, in_sem.at[0]),
@@ -68,13 +76,6 @@
     ]
     for copy in loads:
         copy.start()
-
-    for number, (axis, halo) in enumerate((("gx", hx_v), ("gy", hy_v), ("gz", hz_v))):
-        for side in range(2):
-            @pl.when(at[axis] == (0 if side == 0 else sizes[axis] - 1))
-            def _():
-                for turn in range(2):
-                    halo[turn, side] = jnp.zeros(halo.shape[2:], F32)
 
     def greet(semaphore):
         for k in range(1, group):
@@ -97,11 +98,83 @@
     barrier = pltpu.get_barrier_semaphore()
     greet(barrier)
 
+    messages = {"x": [], "z": [], "y": [], "corner": []}
+    for s in range(2):
+        end = (cx - 1) * s
+        messages["x"].append(((("gx", s),), load_v.at[end], lambda s: hx_v.at[s, 0]))
+        messages["x"].append(((("gx", s),), p_v.at[end], lambda s: hx_v.at[s, 1]))
+        messages["y"].append(((("gy", s),), ysend_v.at[s], lambda s: hy_v.at[s]))
+        messages["z"].append(((("gz", s),), zsend_v, lambda s: hz_v.at[s]))
+    for s in range(2):
+        for t in range(2):
+            messages["corner"] += [
+                ((("gx", s), ("gy", t)), xy_v.at[2 * s + t], lambda s, t: hxy_v.at[2 * s + t]),
+                ((("gx", s), ("gz", t)), xz_v, lambda s, t: hxz_v.at[2 * s + t]),
+                ((("gy", s), ("gz", t)), yz_v.at[s], lambda s, t: hyz_v.at[2 * s + t]),
+            ]
+    number = {}
+    for name, group_of in messages.items():
+        for order, (sides, _, _) in enumerate(group_of):
+            number[name, order] = len(number)
+
+    def opposite(name, order):
+        sides = messages[name][order][0]
+        width = {"x": 2, "y": 1, "z": 1, "corner": 3}[name]
+        flipped = 0
+        for _, side in sides:
+            flipped = 2 * flipped + 1 - side
+        return width * flipped + order % width
+
+    def message(name, order):
+        sides, src, place = messages[name][order]
+        back = number[name, opposite(name, order)]
+        return pltpu.make_async_remote_copy(
+            src_ref=src, dst_ref=place(*[1 - side for _, side in sides]),
+            send_sem=halo_send.at[number[name, order]], recv_sem=halo_recv.at[back],
+            device_id={
+                axis: lax.rem(at[axis] + (1 if side else sizes[axis] - 1), sizes[axis])
+                for axis, side in sides
+            },
+            device_id_type=MESH,
+        )
+
+    def each(name, act):
+        for order, (sides, _, _) in enumerate(messages[name]):
+            @pl.when(near_all(sides))
+            def _():
+                act(name, order)
+
+    def send(name):
+        each(name, lambda name, order: message(name, order).start())
+
+    def receive(name):
+        each(name, lambda name, order: message(name, opposite(name, order)).wait_recv())
+
+    def finish(name):
+        each(name, lambda name, order: message(name, order).wait_send())
+
+    for name in messages:
+        for sides, _, place in messages[name]:
+            slot = place(*[side for _, side in sides])
+
+            @pl.when(jnp.logical_not(near_all(sides)))
+            def _():
+                slot[...] = jnp.zeros(slot.shape, F32)
+
     lane = lax.broadcasted_iota(jnp.int32, (cy, cz), 1)
     lane1 = lax.broadcasted_iota(jnp.int32, (1, cz), 1)
     lane8 = lax.broadcasted_iota(jnp.int32, (8, cz), 1)
     row = lax.broadcasted_iota(jnp.int32, (cy, cz), 0)
+    row8 = lax.broadcasted_iota(jnp.int32, (8, cz), 0)
+    layer = lax.broadcasted_iota(jnp.int32, (cx, cz), 0)
+    lane_x = lax.broadcasted_iota(jnp.int32, (cx, cz), 1)
     right_half = lane >= cz // 2
+    odd = lane % 2 == 1
+    ends = (lane == 0) | (lane == cz - 1)
+
+    def turn(values, by, axis=1):
+        by = by % values.shape[axis]
+        return values if by == 0 else pltpu.roll(values, by, axis=axis)
 
     loads[0].wait()
     for copy in loads[3:]:
@@ -151,162 +224,225 @@
     pl.semaphore_wait(barrier, greeted)
     exchanges = []
     for k in range(1, group):
-        for number, (src, dst) in enumerate(((send_v, recv_v), (stag_v, rtag_v))):
+        for order, (src, dst) in enumerate(((send_v, recv_v), (stag_v, rtag_v))):
             copy = pltpu.make_async_remote_copy(
                 src_ref=src.at[k], dst_ref=dst.at[k],
-                send_sem=a2a_send.at[number, k], recv_sem=a2a_recv.at[number, k],
+                send_sem=a2a_send.at[order, k], recv_sem=a2a_recv.at[order, k],
                 device_id=beside({"gx": k}), device_id_type=MESH,
             )
             copy.start()
             exchanges.append(copy)
-    for relay in range(relays - 1):
-        greet(relay_sem.at[relay])
-        pl.semaphore_wait(relay_sem.at[relay], greeted)
-    greet(relay_sem.at[relays - 1])
+    greet(relay_sem.at[0])
     loads[1].wait()
     loads[2].wait()
+
+    for x in range(cx):
+        for place, y in enumerate((0, 1, cy - 2, cy - 1)):
+            rows_v[place, x:x + 1] = load_v[x, y:y + 1]
+        for place, y in enumerate((0, cy - 1)):
+            drows_v[place, x:x + 1] = diag_v[x, y:y + 1]
+    outer, inner, outer_diag = (jnp.zeros((cy, cz), F32) for _ in range(3))
+    for x in range(cx):
+        plane = load_v[x]
+        mine = lane // 2 == x
+        outer = jnp.where(mine, turn(plane, 2 * x + 1), outer)
+        outer_diag = jnp.where(mine, turn(diag_v[x], 2 * x + 1), outer_diag)
+        second = jnp.where(odd, turn(plane, 2 * x), turn(plane, 2 * x + 2))
+        inner = jnp.where(mine, second, inner)
+    cols_v[0], cols_v[1], cols_v[2] = outer, inner, outer_diag
+
+    for relay in range(relays):
+        pl.semaphore_wait(relay_sem.at[relay], greeted)
+        if relay < relays - 1:
+            greet(relay_sem.at[relay + 1])
     for copy in exchanges:
         copy.wait_recv()
 
     for k in range(group):
         turned_v[k] = pltpu.roll(recv_v[k], cz // 2, axis=1)
-    tags_of = [rtag_v[k] for k in range(group)]
-    turned_tags = [
-        pltpu.roll(jnp.broadcast_to(tags, (8, cz)), cz // 2, axis=1)[:1] for tags in tags_of
-    ]
-    want = [(2 * x + jnp.where(lane1 >= cz // 2, 1, 0)).astype(F32) for x in range(cx)]
-    order = [0, cx - 1] + list(range(1, cx - 1))
-
-    def halo_copy(turn, axis, side, src):
-        number, halo = AXES.index(axis), (hx_v, hy_v, hz_v)[AXES.index(axis)]
-        step = sizes[axis] - 1 if side == 0 else 1
-        return pltpu.make_async_remote_copy(
-            src_ref=src, dst_ref=halo.at[turn, 1 - side],
-            send_sem=halo_send.at[turn, 2 * number + side],
-            recv_sem=halo_recv.at[turn, 2 * number + 1 - side],
-            device_id={axis: lax.rem(at[axis] + step, sizes[axis])}, device_id_type=MESH,
-        )
-
-    def faces(turn, field, axis):
-        if axis == "gx":
-            return field.at[0], field.at[cx - 1]
-        if axis == "gy":
-            return ysend_v.at[turn, 0], ysend_v.at[turn, 1]
-        return zsend_v.at[turn], zsend_v.at[turn]
-
-    def send(turn, field, axis):
-        for side in range(2):
-            @pl.when(near(axis, side))
-            def _():
-                halo_copy(turn, axis, side, faces(turn, field, axis)[side]).start()
-
-    def receive(turn, field, axis):
-        for side in range(2):
-            @pl.when(near(axis, side))
-            def _():
-                halo_copy(turn, axis, 1 - side, faces(turn, field, axis)[1 - side]).wait_recv()
-
-    def finish(turn, field, axis):
-        for side in range(2):
-            @pl.when(near(axis, side))
-            def _():
-                halo_copy(turn, axis, side, faces(turn, field, axis)[side]).wait_send()
-
-    def pack(turn, x, plane, packed):
-        ysend_v[turn, 0, x:x + 1] = plane[:1]
-        ysend_v[turn, 1, x:x + 1] = plane[cy - 1:]
-        turned = plane if x == 0 else pltpu.roll(plane, 2 * x, axis=1)
-        return jnp.where(((lane + 1) % cz) // 2 == x, turned, packed)
-
-    packed = jnp.zeros((cy, cz), F32)
-    for x in order:
+    sources = []
+    for k in range(group):
+        tags = rtag_v[k]
+        swapped = pltpu.roll(jnp.broadcast_to(tags, (8, cz)), cz // 2, axis=1)[:1]
+        sources += [(recv_v.at[k], tags), (turned_v.at[k], swapped)]
+    half1 = jnp.where(lane1 >= cz // 2, 1, 0)
+
+    def scatter(x):
+        want = (2 * x + half1).astype(F32)
         plane = load_v[x]
-        for k in range(group):
-            plane = plane + jnp.where(tags_of[k] == want[x], recv_v[k], 0.0)
-            plane = plane + jnp.where(turned_tags[k] == want[x], turned_v[k], 0.0)
+        for values, tags in sources:
+            plane = plane + jnp.where(tags == want, values[...], 0.0)
         load_v[x] = plane
-        packed = pack(0, x, plane, packed)
-        if x == cx - 1:
-            send(0, load_v, "gx")
-    zsend_v[0] = packed
-    send(0, load_v, "gz")
-    send(0, load_v, "gy")
-
-    def inside(src, dst):
-        for x in range(cx):
-            plane = src[x]
-            around = jnp.where(lane == 0, 0.0, pltpu.roll(plane, 1, axis=1))
-            around = around + jnp.where(lane == cz - 1, 0.0, pltpu.roll(plane, cz - 1, axis=1))
-            around = around + jnp.where(row == 0, 0.0, pltpu.roll(plane, 1, axis=0))
-            around = around + jnp.where(row == cy - 1, 0.0, pltpu.roll(plane, cy - 1, axis=0))
-            if x > 0:
-                around = around + src[x - 1]
-            if x < cx - 1:
-                around = around + src[x + 1]
-            dst[x] = diag_v[x] * plane - around
+
+    def inside(src, x):
+        plane = src[x]
+        around = jnp.where(lane == 0, 0.0, pltpu.roll(plane, 1, axis=1))
+        around = around + jnp.where(lane == cz - 1, 0.0, pltpu.roll(plane, cz - 1, axis=1))
+        around = around + jnp.where(row == 0, 0.0, pltpu.roll(plane, 1, axis=0))
+        around = around + jnp.where(row == cy - 1, 0.0, pltpu.roll(plane, cy - 1, axis=0))
+        if x > 0:
+            around = around + src[x - 1]
+        if x < cx - 1:
+            around = around + src[x + 1]
+        return diag_v[x] * plane - around
+
+    for x in (0, 1, cx - 2, cx - 1):
+        scatter(x)
+    for x in (0, cx - 1):
+        p_v[x] = inside(load_v, x)
+    send("x")
+
+    want = (2 * layer + jnp.where(lane_x >= cz // 2, 1, 0)).astype(F32)
+    faces = [rows_v[place] for place in range(4)]
+    for values, tags in sources:
+        hit = jnp.broadcast_to(tags, (cx, cz)) == want
+        for place, y in enumerate((0, 1, cy - 2, cy - 1)):
+            spread = jnp.broadcast_to(values[y:y + 1], (cx, cz))
+            faces[place] = faces[place] + jnp.where(hit, spread, 0.0)
+    for side in range(2):
+        face, second = faces[3 * side], faces[1 + side]
+        around = jnp.where(lane_x == 0, 0.0, pltpu.roll(face, 1, axis=1)) + second
+        around = around + jnp.where(lane_x == cz - 1, 0.0, pltpu.roll(face, cz - 1, axis=1))
+        around = around + jnp.where(layer == 0, 0.0, pltpu.roll(face, 1, axis=0))
+        around = around + jnp.where(layer == cx - 1, 0.0, pltpu.roll(face, cx - 1, axis=0))
+        ysend_v[side, 0] = face
+        ysend_v[side, 1] = drows_v[side] * face - around
+        for s in range(2):
+            xy_v[2 * s + side] = face[(cx - 1) * s:(cx - 1) * s + 1]
+    send("y")
+
+    outer, inner = cols_v[0], cols_v[1]
+    own_tile = (lane + 1 - 2 * (lane % 2)).astype(F32)
+    for values, tags in sources:
+        first = jnp.broadcast_to(tags[:, :1], (1, cz))
+        last = jnp.broadcast_to(tags[:, cz - 1:], (1, cz))
+        tag = jnp.where(lane1 % 2 == 1, first, last)
+        hit = jnp.broadcast_to(tag, (cy, cz)) == own_tile
+        field = values[...]
+        for depth in range(2):
+            low_z = jnp.broadcast_to(field[:, depth:depth + 1], (cy, cz))
+            high_z = jnp.broadcast_to(field[:, cz - 1 - depth:cz - depth], (cy, cz))
+            added = jnp.where(hit, jnp.where(odd, low_z, high_z), 0.0)
+            if depth == 0:
+                outer = outer + added
+            else:
+                inner = inner + added
+    cols_v[0] = outer
+    around = jnp.where(row == 0, 0.0, pltpu.roll(outer, 1, axis=0)) + inner
+    around = around + jnp.where(row == cy - 1, 0.0, pltpu.roll(outer, cy - 1, axis=0))
+    around = around + jnp.where(lane < 2, 0.0, turn(outer, 2))
+    around = around + jnp.where(lane >= 2 * cx - 2, 0.0, turn(outer, -2))
+    image = cols_v[2] * outer - around
+    both = jnp.where(lane < 2 * cx, outer, turn(image, 2 * cx))
+    both = jnp.where(lane < 4 * cx, both, 0.0)
+    rows = cy // folds
+    folded = both[:rows]
+    for part in range(1, folds):
+        folded = folded + turn(both[part * rows:(part + 1) * rows], 4 * cx * part)
+    zsend_v[...] = folded
+    send("z")
+    edge = jnp.zeros((8, cz), F32)
+    for part in range(cy // 8):
+        piece = outer[8 * part:8 * part + 8]
+        piece = jnp.where(lane8 < 2, piece, turn(piece, 4 - 2 * cx))
+        edge = jnp.where(lane8 // 4 == part, turn(piece, 4 * part), edge)
+    xz_v[...] = edge
+    yz_v[0], yz_v[1] = outer[:1], outer[cy - 1:]
+    send("corner")
 
     def fold(acc, values):
         for part in range(cy // 8):
             acc = acc + values[8 * part:8 * part + 8]
         return acc
 
-    def border(turn, src, dst, sink):
-        for axis in ("gx", "gz", "gy"):
-            receive(turn, src, axis)
-        ahead, behind = hz_v[turn, 1], pltpu.roll(hz_v[turn, 0], 2, axis=1)
-        merged = jnp.where(lane % 2 == 0, ahead, behind)
-        for x in order:
-            edge = pltpu.roll(merged, cz - 2 * x - 1, axis=1)
-            plane = dst[x] - jnp.where((lane == 0) | (lane == cz - 1), edge, 0.0)
-            plane = plane - jnp.where(row == 0, hy_v[turn, 0, x:x + 1], 0.0)
-            plane = plane - jnp.where(row == cy - 1, hy_v[turn, 1, x:x + 1], 0.0)
-            if x == 0:
-                plane = plane - hx_v[turn, 0]
-            if x == cx - 1:
-                plane = plane - hx_v[turn, 1]
-            dst[x] = plane
-            sink(x, plane)
-
-    pl.semaphore_wait(relay_sem.at[relays - 1], greeted)
-    inside(load_v, p_v)
-    state = {"packed": jnp.zeros((cy, cz), F32)}
-
-    def first(x, plane):
-        state["packed"] = pack(1, x, plane, state["packed"])
-        if x == cx - 1:
-            send(1, p_v, "gx")
-
-    border(0, load_v, p_v, first)
-    zsend_v[1] = state["packed"]
-    send(1, p_v, "gz")
-    send(1, p_v, "gy")
-    inside(p_v, q_v)
+    for x in range(2, cx - 2):
+        scatter(x)
+    for x in range(1, cx - 1):
+        p_v[x] = inside(load_v, x)
     acc = [jnp.zeros((8, cz), F32) for _ in range(4)]
     for x in range(cx):
-        load, p = load_v[x], p_v[x]
-        acc[0], acc[1], acc[2] = fold(acc[0], load * load), fold(acc[1], load * p), fold(acc[2], p * p)
-
-    def second(x, plane):
+        acc[0] = fold(acc[0], load_v[x] * load_v[x])
+
+    def rim(plane, first, last):
+        top = plane[:8] - jnp.where(row8 == 0, first, 0.0)
+        bottom = plane[cy - 8:] - jnp.where(row8 == 7, last, 0.0)
+        return jnp.concatenate([top, plane[8:cy - 8], bottom], axis=0)
+
+    for name in ("x", "y", "z"):
+        receive(name)
+    finish("x")
+    lane_f = lax.broadcasted_iota(jnp.int32, (rows, cz), 1)
+    merged = jnp.where(lane_f % 2 == 0, hz_v[0], turn(hz_v[1], -2))
+    for x in range(cx):
+        sides = jnp.concatenate([turn(merged, -4 * cx * f - 2 * x) for f in range(folds)], axis=0)
+        plane = p_v[x] - jnp.where(ends, sides, 0.0)
+        plane = rim(plane, hy_v[0, 0, x:x + 1], hy_v[1, 0, x:x + 1])
+        if x == 0:
+            plane = plane - hx_v[0, 0]
+        if x == cx - 1:
+            plane = plane - hx_v[1, 0]
+        p_v[x] = plane
+        acc[1] = fold(acc[1], plane * load_v[x])
+        acc[2] = fold(acc[2], plane * plane)
+    for x in range(cx):
+        q_v[x] = inside(p_v, x)
+
+    receive("corner")
+    there = {
+        (axis, side): jnp.where(near(axis, side), 1.0, 0.0) for axis in AXES for side in range(2)
+    }
+    y_halo = []
+    for side in range(2):
+        halo = hy_v[side, 1] - there["gy", side] * ysend_v[side, 0]
+        halo = halo - jnp.where(layer == 0, 2.0 * hxy_v[side], 0.0)
+        y_halo.append(halo - jnp.where(layer == cx - 1, 2.0 * hxy_v[2 + side], 0.0))
+    z_halo = jnp.concatenate([turn(merged, -4 * cx * f - 2 * cx) for f in range(folds)], axis=0)
+    own = jnp.where(odd, there["gz", 1], there["gz", 0])
+    z_halo = z_halo - own * turn(cols_v[0], -1)
+    even1 = lane1 % 2 == 0
+    z_halo = rim(z_halo, *(
+        2.0 * jnp.where(
+            even1, hyz_v[2 * side],
+            turn(jnp.broadcast_to(hyz_v[2 * side + 1], (8, cz)), -2)[:1],
+        )
+        for side in range(2)
+    ))
+    code = lane8 % 4
+    behind = jnp.where(code == 2, hxz_v[0], hxz_v[2])
+    ahead = turn(jnp.where(code == 3, hxz_v[1], hxz_v[3]), -2)
+    edge = jnp.where(lane8 % 2 == 0, behind, ahead)
+    pieces = []
+    for part in range(cy // 8):
+        first = turn(edge, -4 * part - 2)
+        last = turn(edge, 2 * cx - 2 - 4 * part)
+        added = jnp.where((lane8 == 0) | (lane8 == cz - 1), first, 0.0)
+        added = jnp.where((lane8 == 2 * cx - 2) | (lane8 == 2 * cx - 3), last, added)
+        pieces.append(z_halo[8 * part:8 * part + 8] - 2.0 * added)
+    z_halo = jnp.concatenate(pieces, axis=0)
+    for x in range(cx):
+        plane = q_v[x] - jnp.where(ends, turn(z_halo, -2 * x), 0.0)
+        plane = rim(plane, y_halo[0][x:x + 1], y_halo[1][x:x + 1])
+        for side in range(2):
+            if x == (cx - 1) * side:
+                plane = plane - hx_v[side, 1] + there["gx", side] * load_v[x]
+        q_v[x] = plane
         acc[3] = fold(acc[3], plane * p_v[x])
 
-    border(1, p_v, q_v, second)
-
-    row8 = lax.broadcasted_iota(jnp.int32, (8, cz), 0)
     mine = jnp.zeros((8, cz), F32)
-    for number in range(4):
-        mine = jnp.where(row8 == number, jnp.sum(acc[number], axis=0, keepdims=True), mine)
+    for order in range(4):
+        mine = jnp.where(row8 == order, jnp.sum(acc[order], axis=0, keepdims=True), mine)
     mine = mine + pltpu.roll(mine, cz // 2, axis=1)
     mine = mine + pltpu.roll(mine, cz // 4, axis=1)
     own = row8 == lane8 // (cz // 4)
     mine = jnp.sum(jnp.where(own, mine, 0.0), axis=0, keepdims=True)
     slot = 0
     waiting = []
-    for number, axes in enumerate(stages):
-        part_v[number] = mine
+    for order, axes in enumerate(stages):
+        part_v[order] = mine
         copies = []
         for offset in offsets_of(sizes, axes):
             copy = pltpu.make_async_remote_copy(
-                src_ref=part_v.at[number], dst_ref=gath_v.at[slot],
+                src_ref=part_v.at[order], dst_ref=gath_v.at[slot],
                 send_sem=red_send.at[slot], recv_sem=red_recv.at[slot],
                 device_id=beside(offset), device_id_type=MESH,
             )
@@ -331,13 +467,12 @@
     b = norm / curve
     x_load, x_p = a + b * e, b * a
     r_load, r_p, r_q = c - 6.0 * b * e, a + b * (e - 6.0 * a), b * a
-    for number, value in enumerate((x_load, x_p, r_load, r_p, r_q)):
-        coef_ref[number:number + 1] = jnp.broadcast_to(value, (1, cz))
+    for order, value in enumerate((x_load, x_p, r_load, r_p, r_q)):
+        coef_ref[order:order + 1] = jnp.broadcast_to(value, (1, cz))
     for copy in exchanges + waiting:
         copy.wait_send()
-    for turn, field in ((0, load_v), (1, p_v)):
-        for axis in AXES:
-            finish(turn, field, axis)
+    for name in ("y", "z", "corner"):
+        finish(name)
 
 
 def combine(load_ref, p_ref, q_ref, coef_ref, x_hbm, r_hbm, x_v, r_v, sem):
@@ -377,6 +512,7 @@
     blocks = face_blocks.shape[3]
     cx, cy, cz = right_side.shape
     group = sizes["gx"]
+    folds = cz // (4 * cx)
     stages = stages_of(sizes)
     relays = relays_of(sizes, stages)
     slots = sum(len(offsets_of(sizes, axes)) for axes in stages)
@@ -399,19 +535,28 @@
             pltpu.VMEM((group, cy, cz), F32),
             pltpu.VMEM((group, 1, cz), F32),
             pltpu.VMEM((group, cy, cz), F32),
+            pltpu.VMEM((4, cx, cz), F32),
+            pltpu.VMEM((2, cx, cz), F32),
+            pltpu.VMEM((3, cy, cz), F32),
             pltpu.VMEM((2, 2, cy, cz), F32),
             pltpu.VMEM((2, 2, cx, cz), F32),
             pltpu.VMEM((2, 2, cx, cz), F32),
-            pltpu.VMEM((2, cy, cz), F32),
-            pltpu.VMEM((2, 2, cy, cz), F32),
+            pltpu.VMEM((cy // folds, cz), F32),
+            pltpu.VMEM((2, cy // folds, cz), F32),
+            pltpu.VMEM((4, 1, cz), F32),
+            pltpu.VMEM((4, 1, cz), F32),
+            pltpu.VMEM((2, 1, cz), F32),
+            pltpu.VMEM((4, 1, cz), F32),
+            pltpu.VMEM((8, cz), F32),
+            pltpu.VMEM((4, 8, cz), F32),
             pltpu.VMEM((len(stages), 1, cz), F32),
             pltpu.VMEM((slots, 1, cz), F32),
             pltpu.SemaphoreType.DMA((6,)),
             pltpu.SemaphoreType.DMA((2, group)),
             pltpu.SemaphoreType.DMA((2, group)),
             pltpu.SemaphoreType.REGULAR((relays,)),
-            pltpu.SemaphoreType.DMA((2, 6)),
-            pltpu.SemaphoreType.DMA((2, 6)),
+            pltpu.SemaphoreType.DMA((20,)),
+            pltpu.SemaphoreType.DMA((20,)),
             pltpu.SemaphoreType.DMA((slots,)),
             pltpu.SemaphoreType.DMA((slots,)),
         ],

time: 24.2 us -> 21.6 us (0.89)
  Pallas kernels: 22.7 us -> 20.2 us
    pallas_call x1, Pallas kernels: 21.7 us -> 19.2 us  [per_device(): pl.pallas_call(functools.partial(kernel, sizes, stages, relays), out_shap...]
where the time goes in v3:
time: 21.6 us; the launch traced here: 21.5 us
  Pallas kernels  20.2 us (94%)
  between operations  1.28 us (6%)
    pallas_call x1, Pallas kernels, per_device(): pl.pallas_call(functools.partial(kernel, sizes, stages, relays), out_shap...  19.2 us
    pallas_call x1, Pallas kernels, combined(): pl.pallas_call(combine, out_shape=(box, box), in_specs=[vmem] * 4, out_sp...  1.05 us

profile of v3, /device:TPU:0, one launch (start us, length us, event | category | flops | bytes accessed | tf_op | source)
XLA Modules:
  0.0 21.5 jit_solution(18072282977169283527)
XLA Ops:
  1.3 19.2 %shard_map.77 = (f32[16,64,128]{2,1,0:T(8,128)S(1)}, f32[16,64,128]{2,1,0:T(8,128)S(1)}, f32[16,64,128]{2,1,0:T(8,128)S(1)}, f32[8,128]{1,0:T(8,128)S(1)}) custom-call(s32[6]{0:T(128)} %bitcast.4, s32[6]{0:T(128)} %bitcast.5, s32[1,1,1]{2,1,0:T(1,128)S(6)} %copy.8.live_hbm, f32[6,128,128]{2,1,0:T(8,128)} %bitcast.3, f32[16,64,128]{2,1,0:T(8,128)} %right_hbm.1, ...), custom_call_target="tpu_custom_call" | custom-call | tf_op jit(solution)/shard_map/pallas_call | solution.py:521
  20.4 1.0 %shard_map.78 = (f32[16,64,128]{2,1,0:T(8,128)}, f32[16,64,128]{2,1,0:T(8,128)}) custom-call(f32[16,64,128]{2,1,0:T(8,128)S(1)} %get-tuple-element.6.load_ref, f32[16,64,128]{2,1,0:T(8,128)S(1)} %get-tuple-element.7.p_ref, f32[16,64,128]{2,1,0:T(8,128)S(1)} %get-tuple-element.8.q_ref, f32[8,128]{1,0:T(8,128)S(1)} %get-tuple-element.9.coef_ref), custom_call_target="tpu_custom_call" | custom-call | tf_op jit(solution)/shard_map/pallas_call | solution.py:502

commit v4 on v3

--- a/solution.py
+++ b/solution.py
@@ -98,60 +98,61 @@
     barrier = pltpu.get_barrier_semaphore()
     greet(barrier)
 
-    messages = {"x": [], "z": [], "y": [], "corner": []}
+    messages = {"x": [], "z": [], "y": [], "xy": [], "xz": [], "yz": []}
+    places = {"x": hx_v, "y": hy_v, "z": hz_v, "xy": hxy_v, "xz": hxz_v, "yz": hyz_v}
+    kinds = list(messages)
     for s in range(2):
         end = (cx - 1) * s
         messages["x"].append(((("gx", s),), load_v.at[end], lambda s: hx_v.at[s, 0]))
         messages["x"].append(((("gx", s),), p_v.at[end], lambda s: hx_v.at[s, 1]))
         messages["y"].append(((("gy", s),), ysend_v.at[s], lambda s: hy_v.at[s]))
         messages["z"].append(((("gz", s),), zsend_v, lambda s: hz_v.at[s]))
-    for s in range(2):
         for t in range(2):
-            messages["corner"] += [
-                ((("gx", s), ("gy", t)), xy_v.at[2 * s + t], lambda s, t: hxy_v.at[2 * s + t]),
-                ((("gx", s), ("gz", t)), xz_v, lambda s, t: hxz_v.at[2 * s + t]),
-                ((("gy", s), ("gz", t)), yz_v.at[s], lambda s, t: hyz_v.at[2 * s + t]),
-            ]
-    number = {}
-    for name, group_of in messages.items():
-        for order, (sides, _, _) in enumerate(group_of):
-            number[name, order] = len(number)
-
-    def opposite(name, order):
-        sides = messages[name][order][0]
-        width = {"x": 2, "y": 1, "z": 1, "corner": 3}[name]
-        flipped = 0
-        for _, side in sides:
-            flipped = 2 * flipped + 1 - side
-        return width * flipped + order % width
-
-    def message(name, order):
-        sides, src, place = messages[name][order]
-        back = number[name, opposite(name, order)]
-        return pltpu.make_async_remote_copy(
-            src_ref=src, dst_ref=place(*[1 - side for _, side in sides]),
-            send_sem=halo_send.at[number[name, order]], recv_sem=halo_recv.at[back],
-            device_id={
-                axis: lax.rem(at[axis] + (1 if side else sizes[axis] - 1), sizes[axis])
-                for axis, side in sides
-            },
-            device_id_type=MESH,
-        )
-
-    def each(name, act):
-        for order, (sides, _, _) in enumerate(messages[name]):
+            messages["xy"].append(
+                ((("gx", s), ("gy", t)), xy_v.at[2 * s + t], lambda s, t: hxy_v.at[2 * s + t])
+            )
+            messages["xz"].append(
+                ((("gx", s), ("gz", t)), xz_v, lambda s, t: hxz_v.at[2 * s + t])
+            )
+            messages["yz"].append(
+                ((("gy", s), ("gz", t)), yz_v.at[s], lambda s, t: hyz_v.at[2 * s + t])
+            )
+
+    def send(name):
+        for sides, src, place in messages[name]:
             @pl.when(near_all(sides))
             def _():
-                act(name, order)
-
-    def send(name):
-        each(name, lambda name, order: message(name, order).start())
+                pltpu.make_async_remote_copy(
+                    src_ref=src, dst_ref=place(*[1 - side for _, side in sides]),
+                    send_sem=halo_send.at[kinds.index(name)],
+                    recv_sem=halo_recv.at[kinds.index(name)],
+                    device_id={
+                        axis: lax.rem(at[axis] + (1 if side else sizes[axis] - 1), sizes[axis])
+                        for axis, side in sides
+                    },
+                    device_id_type=MESH,
+                ).start()
+
+    def settle(name, act):
+        count = jnp.int32(1)
+        for axis, _ in messages[name][0][0]:
+            count = count * sum(jnp.where(near(axis, side), 1, 0) for side in range(2))
+        for found in (1, 2, 4)[:places[name].shape[0] // 2 + 1]:
+            @pl.when(count == found)
+            def _():
+                slots = places[name].at[pl.ds(0, found)]
+                act(pltpu.make_async_remote_copy(
+                    src_ref=slots, dst_ref=slots,
+                    send_sem=halo_send.at[kinds.index(name)],
+                    recv_sem=halo_recv.at[kinds.index(name)],
+                    device_id=beside({"gx": 1}), device_id_type=MESH,
+                ))
 
     def receive(name):
-        each(name, lambda name, order: message(name, opposite(name, order)).wait_recv())
+        settle(name, lambda copy: copy.wait_recv())
 
     def finish(name):
-        each(name, lambda name, order: message(name, order).wait_send())
+        settle(name, lambda copy: copy.wait_send())
 
     for name in messages:
         for sides, _, place in messages[name]:
@@ -222,16 +223,20 @@
         (rtag_v if k == 0 else stag_v)[k] = tags
 
     pl.semaphore_wait(barrier, greeted)
-    exchanges = []
+    boxes = ((send_v, recv_v), (stag_v, rtag_v))
+
+    def exchange(order, slots, k):
+        src, dst = boxes[order]
+        return pltpu.make_async_remote_copy(
+            src_ref=src.at[slots], dst_ref=dst.at[slots],
+            send_sem=a2a_send.at[order], recv_sem=a2a_recv.at[order],
+            device_id=beside({"gx": k}), device_id_type=MESH,
+        )
+
     for k in range(1, group):
-        for order, (src, dst) in enumerate(((send_v, recv_v), (stag_v, rtag_v))):
-            copy = pltpu.make_async_remote_copy(
-                src_ref=src.at[k], dst_ref=dst.at[k],
-                send_sem=a2a_send.at[order, k], recv_sem=a2a_recv.at[order, k],
-                device_id=beside({"gx": k}), device_id_type=MESH,
-            )
-            copy.start()
-            exchanges.append(copy)
+        for order in range(2):
+            exchange(order, pl.ds(k, 1), k).start()
+    arrivals = [exchange(order, pl.ds(1, group - 1), 1) for order in range(2)] if group > 1 else []
     greet(relay_sem.at[0])
     loads[1].wait()
     loads[2].wait()
@@ -255,7 +260,7 @@
         pl.semaphore_wait(relay_sem.at[relay], greeted)
         if relay < relays - 1:
             greet(relay_sem.at[relay + 1])
-    for copy in exchanges:
+    for copy in arrivals:
         copy.wait_recv()
 
     for k in range(group):
@@ -348,7 +353,8 @@
         edge = jnp.where(lane8 // 4 == part, turn(piece, 4 * part), edge)
     xz_v[...] = edge
     yz_v[0], yz_v[1] = outer[:1], outer[cy - 1:]
-    send("corner")
+    for name in ("xy", "xz", "yz"):
+        send(name)
 
     def fold(acc, values):
         for part in range(cy // 8):
@@ -387,7 +393,8 @@
     for x in range(cx):
         q_v[x] = inside(p_v, x)
 
-    receive("corner")
+    for name in ("xy", "xz", "yz"):
+        receive(name)
     there = {
         (axis, side): jnp.where(near(axis, side), 1.0, 0.0) for axis in AXES for side in range(2)
     }
@@ -439,20 +446,24 @@
     waiting = []
     for order, axes in enumerate(stages):
         part_v[order] = mine
-        copies = []
-        for offset in offsets_of(sizes, axes):
-            copy = pltpu.make_async_remote_copy(
-                src_ref=part_v.at[order], dst_ref=gath_v.at[slot],
-                send_sem=red_send.at[slot], recv_sem=red_recv.at[slot],
+        offsets = offsets_of(sizes, axes)
+
+        def part(offset, src, dst):
+            return pltpu.make_async_remote_copy(
+                src_ref=src, dst_ref=dst,
+                send_sem=red_send.at[order], recv_sem=red_recv.at[order],
                 device_id=beside(offset), device_id_type=MESH,
             )
-            copy.start()
-            copies.append((slot, copy))
-            slot += 1
-        for at_slot, copy in copies:
-            copy.wait_recv()
-            mine = mine + gath_v[at_slot]
-        waiting += [copy for _, copy in copies]
+
+        for place, offset in enumerate(offsets):
+            part(offset, part_v.at[order], gath_v.at[slot + place]).start()
+        if offsets:
+            span = gath_v.at[pl.ds(slot, len(offsets))]
+            waiting.append(part(offsets[0], span, span))
+            waiting[-1].wait_recv()
+        for place in range(len(offsets)):
+            mine = mine + gath_v[slot + place]
+        slot += len(offsets)
 
     sums = jnp.sum(jnp.where(own, mine, 0.0), axis=1, keepdims=True)
     s0, s1, s2, s3 = (sums[n:n + 1] for n in range(4))
@@ -469,17 +480,16 @@
     r_load, r_p, r_q = c - 6.0 * b * e, a + b * (e - 6.0 * a), b * a
     for order, value in enumerate((x_load, x_p, r_load, r_p, r_q)):
         coef_ref[order:order + 1] = jnp.broadcast_to(value, (1, cz))
-    for copy in exchanges + waiting:
+    for copy in arrivals + waiting:
         copy.wait_send()
-    for name in ("y", "z", "corner"):
+    for name in ("y", "z", "xy", "xz", "yz"):
         finish(name)
 
 
 def combine(load_ref, p_ref, q_ref, coef_ref, x_hbm, r_hbm, x_v, r_v, sem):
     cx = load_ref.shape[0]
     x_load, x_p, r_load, r_p, r_q = (coef_ref[n:n + 1] for n in range(5))
-    pieces = sem.shape[1]
-    copies = []
+    pieces = 4
     for piece in range(pieces):
         first, last = cx * piece // pieces, cx * (piece + 1) // pieces
         for x in range(first, last):
@@ -488,11 +498,9 @@
             r_v[x] = r_load * load - r_p * p + r_q * q_ref[x]
         span = pl.ds(first, last - first)
         for number, (src, dst) in enumerate(((x_v, x_hbm), (r_v, r_hbm))):
-            copy = pltpu.make_async_copy(src.at[span], dst.at[span], sem.at[number, piece])
-            copy.start()
-            copies.append(copy)
-    for copy in copies:
-        copy.wait()
+            pltpu.make_async_copy(src.at[span], dst.at[span], sem.at[number]).start()
+    for number, (src, dst) in enumerate(((x_v, x_hbm), (r_v, r_hbm))):
+        pltpu.make_async_copy(src, dst, sem.at[number]).wait()
 
 
 def combined(load, p, q, coef):
@@ -504,7 +512,7 @@
         out_shape=(box, box),
         in_specs=[vmem] * 4,
         out_specs=(hbm, hbm),
-        scratch_shapes=[pltpu.VMEM((cx, cy, cz), F32)] * 2 + [pltpu.SemaphoreType.DMA((2, 4))],
+        scratch_shapes=[pltpu.VMEM((cx, cy, cz), F32)] * 2 + [pltpu.SemaphoreType.DMA((2,))],
     )(*(pltpu.with_memory_space_constraint(a, pltpu.VMEM) for a in (load, p, q, coef)))
 
 
@@ -552,13 +560,13 @@
             pltpu.VMEM((len(stages), 1, cz), F32),
             pltpu.VMEM((slots, 1, cz), F32),
             pltpu.SemaphoreType.DMA((6,)),
-            pltpu.SemaphoreType.DMA((2, group)),
-            pltpu.SemaphoreType.DMA((2, group)),
+            pltpu.SemaphoreType.DMA((2,)),
+            pltpu.SemaphoreType.DMA((2,)),
             pltpu.SemaphoreType.REGULAR((relays,)),
-            pltpu.SemaphoreType.DMA((20,)),
-            pltpu.SemaphoreType.DMA((20,)),
-            pltpu.SemaphoreType.DMA((slots,)),
-            pltpu.SemaphoreType.DMA((slots,)),
+            pltpu.SemaphoreType.DMA((6,)),
+            pltpu.SemaphoreType.DMA((6,)),
+            pltpu.SemaphoreType.DMA((len(stages),)),
+            pltpu.SemaphoreType.DMA((len(stages),)),
         ],
         compiler_params=pltpu.CompilerParams(collective_id=0, has_side_effects=True),
     )(

time: 21.6 us -> 20.6 us (0.954)
  Pallas kernels: 20.2 us -> 19.2 us
    pallas_call x1, Pallas kernels: 19.2 us -> 18.2 us  [per_device(): pl.pallas_call(functools.partial(kernel, sizes, stages, relays), out_shap...]
where the time goes in v4:
time: 20.6 us; the launch traced here: 20.5 us
  Pallas kernels  19.2 us (93%)
  between operations  1.28 us (6%)
    pallas_call x1, Pallas kernels, per_device(): pl.pallas_call(functools.partial(kernel, sizes, stages, relays), out_shap...  18.2 us
    pallas_call x1, Pallas kernels, combined(): pl.pallas_call(combine, out_shape=(box, box), in_specs=[vmem] * 4, out_sp...  0.99 us

profile of v4, /device:TPU:0, one launch (start us, length us, event | category | flops | bytes accessed | tf_op | source)
XLA Modules:
  0.0 20.5 jit_solution(9428954574543457042)
XLA Ops:
  1.3 18.2 %shard_map.77 = (f32[16,64,128]{2,1,0:T(8,128)S(1)}, f32[16,64,128]{2,1,0:T(8,128)S(1)}, f32[16,64,128]{2,1,0:T(8,128)S(1)}, f32[8,128]{1,0:T(8,128)S(1)}) custom-call(s32[6]{0:T(128)} %bitcast.4, s32[6]{0:T(128)} %bitcast.5, s32[1,1,1]{2,1,0:T(1,128)S(6)} %copy.8.live_hbm, f32[6,128,128]{2,1,0:T(8,128)} %bitcast.3, f32[16,64,128]{2,1,0:T(8,128)} %right_hbm.1, ...), custom_call_target="tpu_custom_call" | custom-call | tf_op jit(solution)/shard_map/pallas_call | solution.py:529
  19.5 1.0 %shard_map.78 = (f32[16,64,128]{2,1,0:T(8,128)}, f32[16,64,128]{2,1,0:T(8,128)}) custom-call(f32[16,64,128]{2,1,0:T(8,128)S(1)} %get-tuple-element.6.load_ref, f32[16,64,128]{2,1,0:T(8,128)S(1)} %get-tuple-element.7.p_ref, f32[16,64,128]{2,1,0:T(8,128)S(1)} %get-tuple-element.8.q_ref, f32[8,128]{1,0:T(8,128)S(1)} %get-tuple-element.9.coef_ref), custom_call_target="tpu_custom_call" | custom-call | tf_op jit(solution)/shard_map/pallas_call | solution.py:510

commit v5 on v4

--- a/solution.py
+++ b/solution.py
@@ -18,7 +18,10 @@
     found = [()]
     for axis in axes:
         found = [done + (step,) for done in found for step in range(sizes[axis])]
-    return [dict(zip(axes, steps)) for steps in found if any(steps)]
+    offsets = [dict(zip(axes, steps)) for steps in found if any(steps)]
+    return sorted(
+        offsets, key=lambda o: -sum(s if a != "gx" else s / sizes[a] for a, s in o.items())
+    )
 
 
 def stages_of(sizes):
@@ -32,11 +35,12 @@
 
 
 def relays_of(sizes, stages):
-    reach = max(
-        sum(1 if axis == "gx" else sizes[axis] - 1 for axis in axes if sizes[axis] > 1)
-        for axes in stages
-    )
-    return max(1, reach - 2)
+    rounds = 1
+    for axes in stages:
+        steps = [sizes[axis] - 1 for axis in axes if axis != "gx"]
+        single = sum(n % 2 for n in steps) + (1 if "gx" in axes and sizes["gx"] > 1 else 0)
+        rounds = max(rounds, 1 + sum(n // 2 for n in steps) + max(0, single - 3))
+    return rounds
 
 
 def kernel(
@@ -45,13 +49,12 @@
     load_v, p_v, q_v, coef_ref,
     rank_ref, tile_ref, live_ref, face_v, diag_v, sums_v,
     send_v, stag_v, recv_v, rtag_v, turned_v, rows_v, drows_v, cols_v,
-    hx_v, ysend_v, hy_v, zsend_v, hz_v, xy_v, hxy_v, yz_v, hyz_v, xz_v, hxz_v, part_v, gath_v,
+    hx_v, ysend_v, hy_v, zsend_v, hz_v, xy_v, hxy_v, yz_v, hyz_v, xz_v, hxz_v, mix_v, part_v, gath_v,
     in_sem, a2a_send, a2a_recv, relay_sem, halo_send, halo_recv, red_send, red_recv,
 ):
     cx, cy, cz = load_v.shape
     blocks = face_v.shape[0]
     group = sizes["gx"]
-    folds = cy // zsend_v.shape[0]
     at = {axis: lax.axis_index(axis) for axis in AXES}
 
     def near(axis, side):
@@ -59,6 +62,18 @@
 
     def beside(offset):
         return {a: lax.rem(at[a] + s, sizes[a]) for a, s in offset.items() if s}
+
+    def across(offset):
+        where = {}
+        for axis, step in offset.items():
+            if sizes[axis] & (sizes[axis] - 1):
+                where[axis] = lax.rem(at[axis] + step, sizes[axis])
+            else:
+                where[axis] = at[axis]
+                for bit in (1 << n for n in range(sizes[axis].bit_length())):
+                    if step & bit:
+                        where[axis] = where[axis] + bit - 2 * bit * lax.rem(at[axis] // bit, 2)
+        return {axis: index for axis, index in where.items() if offset[axis]}
 
     def near_all(sides):
         found = near(*sides[0])
@@ -77,24 +92,32 @@
     for copy in loads:
         copy.start()
 
-    def greet(semaphore):
+    def within(axis, step):
+        return at[axis] + step >= 0 if step < 0 else at[axis] + step < sizes[axis]
+
+    def greet(semaphore, reach=1):
         for k in range(1, group):
             pl.semaphore_signal(
                 semaphore, inc=1, device_id=beside({"gx": k}), device_id_type=MESH
             )
         for axis in ("gy", "gz"):
-            for side in range(2):
-                @pl.when(near(axis, side))
-                def _():
-                    pl.semaphore_signal(
-                        semaphore, inc=1, device_id={axis: at[axis] + 2 * side - 1},
-                        device_id_type=MESH,
-                    )
-
-    greeted = jnp.int32(group - 1)
-    for axis in ("gy", "gz"):
-        for side in range(2):
-            greeted = greeted + jnp.where(near(axis, side), 1, 0)
+            for step in range(-reach, reach + 1):
+                if 0 < abs(step) < sizes[axis]:
+                    @pl.when(within(axis, step))
+                    def _():
+                        pl.semaphore_signal(
+                            semaphore, inc=1, device_id={axis: at[axis] + step},
+                            device_id_type=MESH,
+                        )
+
+    def greeted(reach=1):
+        count = jnp.int32(group - 1)
+        for axis in ("gy", "gz"):
+            for step in range(-reach, reach + 1):
+                if 0 < abs(step) < sizes[axis]:
+                    count = count + jnp.where(within(axis, step), 1, 0)
+        return count
+
     barrier = pltpu.get_barrier_semaphore()
     greet(barrier)
 
@@ -106,16 +129,16 @@
         messages["x"].append(((("gx", s),), load_v.at[end], lambda s: hx_v.at[s, 0]))
         messages["x"].append(((("gx", s),), p_v.at[end], lambda s: hx_v.at[s, 1]))
         messages["y"].append(((("gy", s),), ysend_v.at[s], lambda s: hy_v.at[s]))
-        messages["z"].append(((("gz", s),), zsend_v, lambda s: hz_v.at[s]))
+        messages["z"].append(((("gz", s),), zsend_v.at[s], lambda s: hz_v.at[s]))
         for t in range(2):
             messages["xy"].append(
                 ((("gx", s), ("gy", t)), xy_v.at[2 * s + t], lambda s, t: hxy_v.at[2 * s + t])
             )
             messages["xz"].append(
-                ((("gx", s), ("gz", t)), xz_v, lambda s, t: hxz_v.at[2 * s + t])
+                ((("gx", s), ("gz", t)), xz_v.at[2 * s + t], lambda s, t: hxz_v.at[2 * s + t])
             )
             messages["yz"].append(
-                ((("gy", s), ("gz", t)), yz_v.at[s], lambda s, t: hyz_v.at[2 * s + t])
+                ((("gy", s), ("gz", t)), yz_v, lambda s, t: hyz_v.at[2 * s + t])
             )
 
     def send(name):
@@ -170,7 +193,6 @@
     layer = lax.broadcasted_iota(jnp.int32, (cx, cz), 0)
     lane_x = lax.broadcasted_iota(jnp.int32, (cx, cz), 1)
     right_half = lane >= cz // 2
-    odd = lane % 2 == 1
     ends = (lane == 0) | (lane == cz - 1)
 
     def turn(values, by, axis=1):
@@ -194,6 +216,17 @@
     rest = whole - high.astype(F32)
     middle = rest.astype(jnp.bfloat16)
     low = (rest - middle.astype(F32)).astype(jnp.bfloat16)
+    column = lax.broadcasted_iota(jnp.int32, (8, cz), 0)
+    column = jnp.where(column < 2, column, cz // 2 - 4 + column)
+    choice = (lax.broadcasted_iota(jnp.int32, (8, cz), 1) // 2 == column) & (column < cz // 2)
+    choice = jnp.where(choice, 0.25, 0.0).astype(jnp.bfloat16)
+
+    def columns_of(values):
+        return lax.dot_general(
+            choice, values, (((1,), (1,)), ((), ())), preferred_element_type=F32
+        )
+
+    columns = columns_of(low) + columns_of(middle) + columns_of(high)
     sums_v[...] = (
         jnp.dot(low, pair, preferred_element_type=F32)
         + jnp.dot(middle, pair, preferred_element_type=F32)
@@ -207,8 +240,17 @@
         for before in range(b):
             count = count + jnp.where((target[before] == target[b]) & alive[before], 1, 0)
         position.append(count)
+    edges = []
+    for b in range(blocks):
+        here = columns[:, b // 2 * cz:b // 2 * cz + cz]
+        there = pltpu.roll(here, cz // 2, axis=1)
+        first, last = (here, there) if b % 2 == 0 else (there, here)
+        even = jnp.where(lane1 < cz // 2, first[0:1], last[1:2])
+        other = jnp.where(lane1 < cz // 2, first[3:4], last[2:3])
+        edges.append(jnp.where(lax.rem(tile_ref[b], 2) == 0, even, other))
     for k in range(group):
         dest = lax.rem(at["gx"] + k, group)
+        outer = [jnp.zeros((1, cz), F32) for _ in range(CAP)]
         total = jnp.zeros((cy, cz), F32)
         tags = jnp.full((1, cz), -1.0, F32)
         for b in range(blocks):
@@ -219,10 +261,12 @@
             tags = jnp.where(weight > 0.5, tag, tags)
             values = sums_v[b * cy:(b + 1) * cy]
             total = total + values * jnp.where(right_half, right, left)
+            outer = [outer[0] + left * edges[b], outer[1] + right * edges[b]]
         (recv_v if k == 0 else send_v)[k] = total
-        (rtag_v if k == 0 else stag_v)[k] = tags
-
-    pl.semaphore_wait(barrier, greeted)
+        for place, values in enumerate([tags] + outer):
+            (rtag_v if k == 0 else stag_v)[3 * k + place] = values
+
+    pl.semaphore_wait(barrier, greeted())
     boxes = ((send_v, recv_v), (stag_v, rtag_v))
 
     def exchange(order, slots, k):
@@ -235,8 +279,11 @@
 
     for k in range(1, group):
         for order in range(2):
-            exchange(order, pl.ds(k, 1), k).start()
-    arrivals = [exchange(order, pl.ds(1, group - 1), 1) for order in range(2)] if group > 1 else []
+            exchange(order, pl.ds(k * (1, 3)[order], (1, 3)[order]), k).start()
+    arrivals = [
+        exchange(order, pl.ds(step, step * (group - 1)), 1)
+        for order, step in enumerate((1, 3)) if group > 1
+    ]
     greet(relay_sem.at[0])
     loads[1].wait()
     loads[2].wait()
@@ -246,20 +293,21 @@
             rows_v[place, x:x + 1] = load_v[x, y:y + 1]
         for place, y in enumerate((0, cy - 1)):
             drows_v[place, x:x + 1] = diag_v[x, y:y + 1]
-    outer, inner, outer_diag = (jnp.zeros((cy, cz), F32) for _ in range(3))
+    upper, lower = jnp.zeros((cy, cz), F32), jnp.zeros((cy, cz), F32)
     for x in range(cx):
-        plane = load_v[x]
-        mine = lane // 2 == x
-        outer = jnp.where(mine, turn(plane, 2 * x + 1), outer)
-        outer_diag = jnp.where(mine, turn(diag_v[x], 2 * x + 1), outer_diag)
-        second = jnp.where(odd, turn(plane, 2 * x), turn(plane, 2 * x + 2))
-        inner = jnp.where(mine, second, inner)
-    cols_v[0], cols_v[1], cols_v[2] = outer, inner, outer_diag
+        plane, weights = load_v[x], diag_v[x]
+        for side in range(2):
+            spot = cx * side + x
+            upper = jnp.where(lane == spot, turn(plane, spot + side), upper)
+            lower = jnp.where(lane == spot, turn(plane, spot + 3 * side - 1), lower)
+            spot = spot + 2 * cx
+            upper = jnp.where(lane == spot, turn(weights, spot + side), upper)
+    cols_v[...] = jnp.concatenate([upper, lower], axis=0).T[:4 * cx]
 
     for relay in range(relays):
-        pl.semaphore_wait(relay_sem.at[relay], greeted)
+        pl.semaphore_wait(relay_sem.at[relay], greeted(min(relay + 1, 2)))
         if relay < relays - 1:
-            greet(relay_sem.at[relay + 1])
+            greet(relay_sem.at[relay + 1], 2)
     for copy in arrivals:
         copy.wait_recv()
 
@@ -267,7 +315,7 @@
         turned_v[k] = pltpu.roll(recv_v[k], cz // 2, axis=1)
     sources = []
     for k in range(group):
-        tags = rtag_v[k]
+        tags = rtag_v[3 * k]
         swapped = pltpu.roll(jnp.broadcast_to(tags, (8, cz)), cz // 2, axis=1)[:1]
         sources += [(recv_v.at[k], tags), (turned_v.at[k], swapped)]
     half1 = jnp.where(lane1 >= cz // 2, 1, 0)
@@ -290,12 +338,6 @@
         if x < cx - 1:
             around = around + src[x + 1]
         return diag_v[x] * plane - around
-
-    for x in (0, 1, cx - 2, cx - 1):
-        scatter(x)
-    for x in (0, cx - 1):
-        p_v[x] = inside(load_v, x)
-    send("x")
 
     want = (2 * layer + jnp.where(lane_x >= cz // 2, 1, 0)).astype(F32)
     faces = [rows_v[place] for place in range(4)]
@@ -314,47 +356,48 @@
         ysend_v[side, 1] = drows_v[side] * face - around
         for s in range(2):
             xy_v[2 * s + side] = face[(cx - 1) * s:(cx - 1) * s + 1]
+    send("xy")
     send("y")
 
-    outer, inner = cols_v[0], cols_v[1]
-    own_tile = (lane + 1 - 2 * (lane % 2)).astype(F32)
-    for values, tags in sources:
-        first = jnp.broadcast_to(tags[:, :1], (1, cz))
-        last = jnp.broadcast_to(tags[:, cz - 1:], (1, cz))
-        tag = jnp.where(lane1 % 2 == 1, first, last)
-        hit = jnp.broadcast_to(tag, (cy, cz)) == own_tile
-        field = values[...]
-        for depth in range(2):
-            low_z = jnp.broadcast_to(field[:, depth:depth + 1], (cy, cz))
-            high_z = jnp.broadcast_to(field[:, cz - 1 - depth:cz - depth], (cy, cz))
-            added = jnp.where(hit, jnp.where(odd, low_z, high_z), 0.0)
-            if depth == 0:
-                outer = outer + added
-            else:
-                inner = inner + added
-    cols_v[0] = outer
-    around = jnp.where(row == 0, 0.0, pltpu.roll(outer, 1, axis=0)) + inner
-    around = around + jnp.where(row == cy - 1, 0.0, pltpu.roll(outer, cy - 1, axis=0))
-    around = around + jnp.where(lane < 2, 0.0, turn(outer, 2))
-    around = around + jnp.where(lane >= 2 * cx - 2, 0.0, turn(outer, -2))
-    image = cols_v[2] * outer - around
-    both = jnp.where(lane < 2 * cx, outer, turn(image, 2 * cx))
-    both = jnp.where(lane < 4 * cx, both, 0.0)
-    rows = cy // folds
-    folded = both[:rows]
-    for part in range(1, folds):
-        folded = folded + turn(both[part * rows:(part + 1) * rows], 4 * cx * part)
-    zsend_v[...] = folded
+    line = lax.broadcasted_iota(jnp.int32, (2 * cx, cz), 0)
+    lane_z = lax.broadcasted_iota(jnp.int32, (2 * cx, cz), 1)
+    own_tile = (2 * (line % cx) + line // cx).astype(F32)
+    turned = cols_v[:2 * cx]
+    for k in range(group):
+        tags = rtag_v[3 * k]
+        for place in range(CAP):
+            tag = tags[:, :1] if place == 0 else tags[:, cz - 1:]
+            hit = jnp.broadcast_to(tag, (2 * cx, cz)) == own_tile
+            values = jnp.broadcast_to(rtag_v[3 * k + 1 + place], (2 * cx, cz))
+            turned = turned + jnp.where(hit, values, 0.0)
+    around = jnp.where(lane_z == 0, 0.0, turn(turned, 1)) + turn(turned, cz // 2)
+    around = around + jnp.where(lane_z == cy - 1, 0.0, turn(turned, -1))
+    around = around + jnp.where(line % cx == 0, 0.0, turn(turned, 1, 0))
+    around = around + jnp.where(line % cx == cx - 1, 0.0, turn(turned, -1, 0))
+    image = cols_v[2 * cx:] * turned - around
+    turned = jnp.where(lane_z < cy, turned, turn(image, cz // 2))
+    for side in range(2):
+        zsend_v[side] = turned[cx * side:cx * side + cx]
     send("z")
-    edge = jnp.zeros((8, cz), F32)
-    for part in range(cy // 8):
-        piece = outer[8 * part:8 * part + 8]
-        piece = jnp.where(lane8 < 2, piece, turn(piece, 4 - 2 * cx))
-        edge = jnp.where(lane8 // 4 == part, turn(piece, 4 * part), edge)
-    xz_v[...] = edge
-    yz_v[0], yz_v[1] = outer[:1], outer[cy - 1:]
-    for name in ("xy", "xz", "yz"):
+    groups = cx // 8
+    tile = jnp.zeros((8, cz), F32)
+    for side in range(2):
+        for part in range(groups):
+            spot = 2 * (groups * side + part)
+            piece = turn(ysend_v[side, 0, 8 * part:8 * part + 8], spot + 1)
+            tile = jnp.where(lane8 // 2 == spot // 2, piece, tile)
+        for s in range(2):
+            spot = cx * side + (cx - 1) * s
+            xz_v[2 * s + side] = turned[spot:spot + 1]
+    yz_v[...] = tile
+    for name in ("yz", "xz"):
         send(name)
+
+    for x in (0, 1, cx - 2, cx - 1):
+        scatter(x)
+    for x in (0, cx - 1):
+        p_v[x] = inside(load_v, x)
+    send("x")
 
     def fold(acc, values):
         for part in range(cy // 8):
@@ -377,11 +420,15 @@
     for name in ("x", "y", "z"):
         receive(name)
     finish("x")
-    lane_f = lax.broadcasted_iota(jnp.int32, (rows, cz), 1)
-    merged = jnp.where(lane_f % 2 == 0, hz_v[0], turn(hz_v[1], -2))
+    def columned(halves):
+        for side in range(2):
+            mix_v[pl.ds(1 - side, cx, stride=2), :] = halves[side]
+        columns = mix_v[...].T
+        return jnp.concatenate([columns, jnp.zeros((cz, cz - 2 * cx), F32)], axis=1)
+
+    l_halo = columned([hz_v[0], hz_v[1]])[:cy]
     for x in range(cx):
-        sides = jnp.concatenate([turn(merged, -4 * cx * f - 2 * x) for f in range(folds)], axis=0)
-        plane = p_v[x] - jnp.where(ends, sides, 0.0)
+        plane = p_v[x] - jnp.where(ends, turn(l_halo, -2 * x - 1), 0.0)
         plane = rim(plane, hy_v[0, 0, x:x + 1], hy_v[1, 0, x:x + 1])
         if x == 0:
             plane = plane - hx_v[0, 0]
@@ -403,31 +450,25 @@
         halo = hy_v[side, 1] - there["gy", side] * ysend_v[side, 0]
         halo = halo - jnp.where(layer == 0, 2.0 * hxy_v[side], 0.0)
         y_halo.append(halo - jnp.where(layer == cx - 1, 2.0 * hxy_v[2 + side], 0.0))
-    z_halo = jnp.concatenate([turn(merged, -4 * cx * f - 2 * cx) for f in range(folds)], axis=0)
-    own = jnp.where(odd, there["gz", 1], there["gz", 0])
-    z_halo = z_halo - own * turn(cols_v[0], -1)
-    even1 = lane1 % 2 == 0
-    z_halo = rim(z_halo, *(
-        2.0 * jnp.where(
-            even1, hyz_v[2 * side],
-            turn(jnp.broadcast_to(hyz_v[2 * side + 1], (8, cz)), -2)[:1],
-        )
-        for side in range(2)
-    ))
-    code = lane8 % 4
-    behind = jnp.where(code == 2, hxz_v[0], hxz_v[2])
-    ahead = turn(jnp.where(code == 3, hxz_v[1], hxz_v[3]), -2)
-    edge = jnp.where(lane8 % 2 == 0, behind, ahead)
-    pieces = []
-    for part in range(cy // 8):
-        first = turn(edge, -4 * part - 2)
-        last = turn(edge, 2 * cx - 2 - 4 * part)
-        added = jnp.where((lane8 == 0) | (lane8 == cz - 1), first, 0.0)
-        added = jnp.where((lane8 == 2 * cx - 2) | (lane8 == 2 * cx - 3), last, added)
-        pieces.append(z_halo[8 * part:8 * part + 8] - 2.0 * added)
-    z_halo = jnp.concatenate(pieces, axis=0)
+    halves = []
+    for side in range(2):
+        halo = hz_v[side] - there["gz", side] * turn(zsend_v[side], cz // 2)
+        for s in range(2):
+            corner = turn(jnp.broadcast_to(hxz_v[2 * s + side], (8, cz)), cz // 2)[:1]
+            halo = halo - jnp.where(layer == (cx - 1) * s, 2.0 * corner, 0.0)
+        parts = []
+        for part in range(groups):
+            piece = halo[8 * part:8 * part + 8]
+            for s in range(2):
+                spot = 2 * (groups * (1 - s) + part) + side
+                goal = cy if s == 0 else 2 * cy - 1
+                corner = turn(hyz_v[2 * s + side], goal - spot)
+                piece = piece - jnp.where(lane8 == goal, 2.0 * corner, 0.0)
+            parts.append(piece)
+        halves.append(jnp.concatenate(parts, axis=0))
+    z_halo = columned(halves)[cy:2 * cy]
     for x in range(cx):
-        plane = q_v[x] - jnp.where(ends, turn(z_halo, -2 * x), 0.0)
+        plane = q_v[x] - jnp.where(ends, turn(z_halo, -2 * x - 1), 0.0)
         plane = rim(plane, y_halo[0][x:x + 1], y_halo[1][x:x + 1])
         for side in range(2):
             if x == (cx - 1) * side:
@@ -452,7 +493,7 @@
             return pltpu.make_async_remote_copy(
                 src_ref=src, dst_ref=dst,
                 send_sem=red_send.at[order], recv_sem=red_recv.at[order],
-                device_id=beside(offset), device_id_type=MESH,
+                device_id=across(offset), device_id_type=MESH,
             )
 
         for place, offset in enumerate(offsets):
@@ -520,7 +561,6 @@
     blocks = face_blocks.shape[3]
     cx, cy, cz = right_side.shape
     group = sizes["gx"]
-    folds = cz // (4 * cx)
     stages = stages_of(sizes)
     relays = relays_of(sizes, stages)
     slots = sum(len(offsets_of(sizes, axes)) for axes in stages)
@@ -539,24 +579,25 @@
             pltpu.VMEM((cx, cy, cz), F32),
             pltpu.VMEM((blocks * cy, cz), F32),
             pltpu.VMEM((group, cy, cz), F32),
-            pltpu.VMEM((group, 1, cz), F32),
+            pltpu.VMEM((3 * group, 1, cz), F32),
             pltpu.VMEM((group, cy, cz), F32),
-            pltpu.VMEM((group, 1, cz), F32),
+            pltpu.VMEM((3 * group, 1, cz), F32),
             pltpu.VMEM((group, cy, cz), F32),
             pltpu.VMEM((4, cx, cz), F32),
             pltpu.VMEM((2, cx, cz), F32),
-            pltpu.VMEM((3, cy, cz), F32),
+            pltpu.VMEM((4 * cx, cz), F32),
             pltpu.VMEM((2, 2, cy, cz), F32),
             pltpu.VMEM((2, 2, cx, cz), F32),
             pltpu.VMEM((2, 2, cx, cz), F32),
-            pltpu.VMEM((cy // folds, cz), F32),
-            pltpu.VMEM((2, cy // folds, cz), F32),
+            pltpu.VMEM((2, cx, cz), F32),
+            pltpu.VMEM((2, cx, cz), F32),
             pltpu.VMEM((4, 1, cz), F32),
-            pltpu.VMEM((4, 1, cz), F32),
-            pltpu.VMEM((2, 1, cz), F32),
             pltpu.VMEM((4, 1, cz), F32),
             pltpu.VMEM((8, cz), F32),
             pltpu.VMEM((4, 8, cz), F32),
+            pltpu.VMEM((4, 1, cz), F32),
+            pltpu.VMEM((4, 1, cz), F32),
+            pltpu.VMEM((2 * cx, cz), F32),
             pltpu.VMEM((len(stages), 1, cz), F32),
             pltpu.VMEM((slots, 1, cz), F32),
             pltpu.SemaphoreType.DMA((6,)),

time: 20.6 us -> 20.4 us (level)
    pallas_call x1, Pallas kernels: 18.2 us -> 18 us  [per_device(): pl.pallas_call(functools.partial(kernel, sizes, stages, relays), out_shap...]
where the time goes in v5:
time: 20.4 us; the launch traced here: 20.2 us
  Pallas kernels  19 us (93%)
  between operations  1.28 us (6%)
    pallas_call x1, Pallas kernels, per_device(): pl.pallas_call(functools.partial(kernel, sizes, stages, relays), out_shap...  18 us
    pallas_call x1, Pallas kernels, combined(): pl.pallas_call(combine, out_shape=(box, box), in_specs=[vmem] * 4, out_sp...  0.99 us

profile of v5, /device:TPU:0, one launch (start us, length us, event | category | flops | bytes accessed | tf_op | source)
XLA Modules:
  0.0 20.2 jit_solution(2448376021377046518)
XLA Ops:
  1.3 18.0 %shard_map.77 = (f32[16,64,128]{2,1,0:T(8,128)S(1)}, f32[16,64,128]{2,1,0:T(8,128)S(1)}, f32[16,64,128]{2,1,0:T(8,128)S(1)}, f32[8,128]{1,0:T(8,128)S(1)}) custom-call(s32[6]{0:T(128)} %bitcast.4, s32[6]{0:T(128)} %bitcast.5, s32[1,1,1]{2,1,0:T(1,128)S(6)} %copy.8.live_hbm, f32[6,128,128]{2,1,0:T(8,128)} %bitcast.3, f32[16,64,128]{2,1,0:T(8,128)} %right_hbm.1, ...), custom_call_target="tpu_custom_call" | custom-call | tf_op jit(solution)/shard_map/pallas_call | solution.py:569
  19.2 1.0 %shard_map.78 = (f32[16,64,128]{2,1,0:T(8,128)}, f32[16,64,128]{2,1,0:T(8,128)}) custom-call(f32[16,64,128]{2,1,0:T(8,128)S(1)} %get-tuple-element.6.load_ref, f32[16,64,128]{2,1,0:T(8,128)S(1)} %get-tuple-element.7.p_ref, f32[16,64,128]{2,1,0:T(8,128)S(1)} %get-tuple-element.8.q_ref, f32[8,128]{1,0:T(8,128)S(1)} %get-tuple-element.9.coef_ref), custom_call_target="tpu_custom_call" | custom-call | tf_op jit(solution)/shard_map/pallas_call | solution.py:551

commit v6 on v5

--- a/solution.py
+++ b/solution.py
@@ -49,7 +49,7 @@
     load_v, p_v, q_v, coef_ref,
     rank_ref, tile_ref, live_ref, face_v, diag_v, sums_v,
     send_v, stag_v, recv_v, rtag_v, turned_v, rows_v, drows_v, cols_v,
-    hx_v, ysend_v, hy_v, zsend_v, hz_v, xy_v, hxy_v, yz_v, hyz_v, xz_v, hxz_v, mix_v, part_v, gath_v,
+    hx_v, xr_v, hxr_v, qrows_v, qcols_v, ysend_v, hy_v, zsend_v, hz_v, xy_v, hxy_v, yz_v, hyz_v, xz_v, hxz_v, mix_v, part_v, gath_v,
     in_sem, a2a_send, a2a_recv, relay_sem, halo_send, halo_recv, red_send, red_recv,
 ):
     cx, cy, cz = load_v.shape
@@ -121,13 +121,16 @@
     barrier = pltpu.get_barrier_semaphore()
     greet(barrier)
 
-    messages = {"x": [], "z": [], "y": [], "xy": [], "xz": [], "yz": []}
-    places = {"x": hx_v, "y": hy_v, "z": hz_v, "xy": hxy_v, "xz": hxz_v, "yz": hyz_v}
+    messages = {"x": [], "z": [], "y": [], "xr": [], "xy": [], "xz": [], "yz": []}
+    places = {
+        "x": hx_v, "y": hy_v, "z": hz_v, "xr": hxr_v, "xy": hxy_v, "xz": hxz_v, "yz": hyz_v,
+    }
     kinds = list(messages)
     for s in range(2):
         end = (cx - 1) * s
         messages["x"].append(((("gx", s),), load_v.at[end], lambda s: hx_v.at[s, 0]))
         messages["x"].append(((("gx", s),), p_v.at[end], lambda s: hx_v.at[s, 1]))
+        messages["xr"].append(((("gx", s),), xr_v.at[s], lambda s: hxr_v.at[s]))
         messages["y"].append(((("gy", s),), ysend_v.at[s], lambda s: hy_v.at[s]))
         messages["z"].append(((("gz", s),), zsend_v.at[s], lambda s: hz_v.at[s]))
         for t in range(2):
@@ -375,6 +378,7 @@
     around = around + jnp.where(line % cx == 0, 0.0, turn(turned, 1, 0))
     around = around + jnp.where(line % cx == cx - 1, 0.0, turn(turned, -1, 0))
     image = cols_v[2 * cx:] * turned - around
+    deeper = turn(turned, cz // 2)
     turned = jnp.where(lane_z < cy, turned, turn(image, cz // 2))
     for side in range(2):
         zsend_v[side] = turned[cx * side:cx * side + cx]
@@ -389,8 +393,10 @@
         for s in range(2):
             spot = cx * side + (cx - 1) * s
             xz_v[2 * s + side] = turned[spot:spot + 1]
+            xr_v[s, 2 * side] = turned[spot:spot + 1]
+            xr_v[s, 2 * side + 1] = deeper[spot:spot + 1]
     yz_v[...] = tile
-    for name in ("yz", "xz"):
+    for name in ("yz", "xz", "xr"):
         send(name)
 
     for x in (0, 1, cx - 2, cx - 1):
@@ -409,38 +415,25 @@
     for x in range(1, cx - 1):
         p_v[x] = inside(load_v, x)
     acc = [jnp.zeros((8, cz), F32) for _ in range(4)]
+    image = jnp.zeros((cy, cz), F32)
     for x in range(cx):
-        acc[0] = fold(acc[0], load_v[x] * load_v[x])
+        load, p, q = load_v[x], p_v[x], inside(p_v, x)
+        q_v[x] = q
+        pairs = ((load, load), (load, p), (p, p), (p, q))
+        acc = [fold(total, one * other) for total, (one, other) in zip(acc, pairs)]
+        for side in range(2):
+            y = (cy - 1) * side
+            qrows_v[side, x:x + 1] = q[y:y + 1]
+            spot = cx * side + x
+            image = jnp.where(lane == spot, turn(q, spot + side), image)
+    qcols_v[...] = jnp.concatenate([image, jnp.zeros((cz - cy, cz), F32)], axis=0).T[:2 * cx]
 
     def rim(plane, first, last):
         top = plane[:8] - jnp.where(row8 == 0, first, 0.0)
         bottom = plane[cy - 8:] - jnp.where(row8 == 7, last, 0.0)
         return jnp.concatenate([top, plane[8:cy - 8], bottom], axis=0)
 
-    for name in ("x", "y", "z"):
-        receive(name)
-    finish("x")
-    def columned(halves):
-        for side in range(2):
-            mix_v[pl.ds(1 - side, cx, stride=2), :] = halves[side]
-        columns = mix_v[...].T
-        return jnp.concatenate([columns, jnp.zeros((cz, cz - 2 * cx), F32)], axis=1)
-
-    l_halo = columned([hz_v[0], hz_v[1]])[:cy]
-    for x in range(cx):
-        plane = p_v[x] - jnp.where(ends, turn(l_halo, -2 * x - 1), 0.0)
-        plane = rim(plane, hy_v[0, 0, x:x + 1], hy_v[1, 0, x:x + 1])
-        if x == 0:
-            plane = plane - hx_v[0, 0]
-        if x == cx - 1:
-            plane = plane - hx_v[1, 0]
-        p_v[x] = plane
-        acc[1] = fold(acc[1], plane * load_v[x])
-        acc[2] = fold(acc[2], plane * plane)
-    for x in range(cx):
-        q_v[x] = inside(p_v, x)
-
-    for name in ("xy", "xz", "yz"):
+    for name in ("x", "xr", "y", "z", "xy", "xz", "yz"):
         receive(name)
     there = {
         (axis, side): jnp.where(near(axis, side), 1.0, 0.0) for axis in AXES for side in range(2)
@@ -466,19 +459,113 @@
                 piece = piece - jnp.where(lane8 == goal, 2.0 * corner, 0.0)
             parts.append(piece)
         halves.append(jnp.concatenate(parts, axis=0))
-    z_halo = columned(halves)[cy:2 * cy]
-    for x in range(cx):
-        plane = q_v[x] - jnp.where(ends, turn(z_halo, -2 * x - 1), 0.0)
-        plane = rim(plane, y_halo[0][x:x + 1], y_halo[1][x:x + 1])
+
+    def add(at_sum, values):
+        for part in range(values.shape[0] // 8):
+            acc[at_sum] = acc[at_sum] + values[8 * part:8 * part + 8]
+
+    def face_sums(h, halo, load, p, q, stencil):
+        add(1, -(load * h))
+        add(2, h * (h - 2.0 * p))
+        add(3, h * (stencil + halo - 2.0 * q) - p * halo)
+
+    rows = [jnp.zeros((1, cz), F32) for _ in range(4)]
+    for side in range(2):
+        x = (cx - 1) * side
+        h, load = hx_v[side, 0], load_v[x]
+        around = jnp.where(lane == 0, 0.0, turn(h, 1))
+        around = around + jnp.where(lane == cz - 1, 0.0, turn(h, -1))
+        around = around + jnp.where(row == 0, 0.0, turn(h, 1, 0))
+        around = around + jnp.where(row == cy - 1, 0.0, turn(h, -1, 0))
+        halo = hx_v[side, 1] - there["gx", side] * load
+        face_sums(h, halo, load, p_v[x], q_v[x], diag_v[x] * h - around)
+    y_stencil = []
+    for side in range(2):
+        h = hy_v[side, 0]
+        around = jnp.where(lane_x == 0, 0.0, turn(h, 1))
+        around = around + jnp.where(lane_x == cz - 1, 0.0, turn(h, -1))
+        around = around + jnp.where(layer == 0, 0.0, turn(h, 1, 0))
+        around = around + jnp.where(layer == cx - 1, 0.0, turn(h, -1, 0))
+        y_stencil.append(drows_v[side] * h - around)
+        face_sums(
+            h, y_halo[side], ysend_v[side, 0], ysend_v[side, 1], qrows_v[side], y_stencil[side]
+        )
+    z_stencil, z_h, z_halves = [], [], []
+    used = lane_x < cy
+    for side in range(2):
+        h = jnp.where(used, hz_v[side], 0.0)
+        halo = jnp.where(used, turn(halves[side], cz // 2), 0.0)
+        around = turn(h, 1) + jnp.where(lane_x == cz - 1, 0.0, turn(h, -1))
+        around = around + jnp.where(layer == 0, 0.0, turn(h, 1, 0))
+        around = around + jnp.where(layer == cx - 1, 0.0, turn(h, -1, 0))
+        span = pl.ds(cx * side, cx)
+        z_stencil.append(cols_v[pl.ds(2 * cx + cx * side, cx)] * h - around)
+        z_h.append(h)
+        z_halves.append(halo)
+        own_p = turn(zsend_v[side], cz // 2)
+        face_sums(h, halo, zsend_v[side], own_p, qcols_v[span], z_stencil[side])
+
+    def edge_sums(one, one_in, one_halo, other, other_halo, other_stencil):
+        second = 2.0 * one * other
+        third = 2.0 * (one * other_stencil - one_in * other)
+        return second, third + one * other_halo + other * one_halo
+
+    for s in range(2):
+        x = (cx - 1) * s
+        for t in range(2):
+            y, y_in = ((0, 1), (cy - 1, cy - 2))[t]
+            second, third = edge_sums(
+                hx_v[s, 0, y:y + 1], hx_v[s, 0, y_in:y_in + 1],
+                hx_v[s, 1, y:y + 1] - there["gx", s] * load_v[x, y:y + 1],
+                hy_v[t, 0, x:x + 1], y_halo[t][x:x + 1], y_stencil[t][x:x + 1],
+            )
+            rows[2], rows[3] = rows[2] + second, rows[3] + third
+            second, third = edge_sums(
+                hxr_v[s, 2 * t], hxr_v[s, 2 * t + 1],
+                turn(jnp.broadcast_to(hxr_v[s, 2 * t], (8, cz)), cz // 2)[:1]
+                - there["gx", s] * zsend_v[t, x:x + 1],
+                z_h[t][x:x + 1], z_halves[t][x:x + 1], z_stencil[t][x:x + 1],
+            )
+            used1 = lane1 < cy
+            rows[2] = rows[2] + jnp.where(used1, second, 0.0)
+            rows[3] = rows[3] + jnp.where(used1, third, 0.0)
+            goal = (cy - 1) * s
+            spot, spot_in = ((0, 1), (cz - 1, cz - 2))[t]
+            second, third = edge_sums(
+                turn(hy_v[s, 0], goal - spot), turn(hy_v[s, 0], goal - spot_in),
+                turn(y_halo[s], goal - spot), z_h[t], z_halves[t], z_stencil[t],
+            )
+            add(2, jnp.where(lane_x == goal, second, 0.0))
+            add(3, jnp.where(lane_x == goal, third, 0.0))
+
+    def columned(halves):
         for side in range(2):
-            if x == (cx - 1) * side:
-                plane = plane - hx_v[side, 1] + there["gx", side] * load_v[x]
-        q_v[x] = plane
-        acc[3] = fold(acc[3], plane * p_v[x])
+            mix_v[pl.ds(1 - side, cx, stride=2), :] = halves[side]
+        columns = mix_v[...].T
+        return jnp.concatenate([columns, jnp.zeros((cz, cz - 2 * cx), F32)], axis=1)
+
+    def complete():
+        finish("x")
+        l_halo = columned([hz_v[0], hz_v[1]])[:cy]
+        for x in range(cx):
+            plane = p_v[x] - jnp.where(ends, turn(l_halo, -2 * x - 1), 0.0)
+            plane = rim(plane, hy_v[0, 0, x:x + 1], hy_v[1, 0, x:x + 1])
+            for side in range(2):
+                if x == (cx - 1) * side:
+                    plane = plane - hx_v[side, 0]
+            p_v[x] = plane
+        z_halo = columned(halves)[cy:2 * cy]
+        for x in range(cx):
+            plane = inside(p_v, x) - jnp.where(ends, turn(z_halo, -2 * x - 1), 0.0)
+            plane = rim(plane, y_halo[0][x:x + 1], y_halo[1][x:x + 1])
+            for side in range(2):
+                if x == (cx - 1) * side:
+                    plane = plane - hx_v[side, 1] + there["gx", side] * load_v[x]
+            q_v[x] = plane
 
     mine = jnp.zeros((8, cz), F32)
     for order in range(4):
-        mine = jnp.where(row8 == order, jnp.sum(acc[order], axis=0, keepdims=True), mine)
+        mine = jnp.where(row8 == order, jnp.sum(acc[order], axis=0, keepdims=True) + rows[order], mine)
     mine = mine + pltpu.roll(mine, cz // 2, axis=1)
     mine = mine + pltpu.roll(mine, cz // 4, axis=1)
     own = row8 == lane8 // (cz // 4)
@@ -498,6 +585,8 @@
 
         for place, offset in enumerate(offsets):
             part(offset, part_v.at[order], gath_v.at[slot + place]).start()
+        if order == 0:
+            complete()
         if offsets:
             span = gath_v.at[pl.ds(slot, len(offsets))]
             waiting.append(part(offsets[0], span, span))
@@ -523,7 +612,7 @@
         coef_ref[order:order + 1] = jnp.broadcast_to(value, (1, cz))
     for copy in arrivals + waiting:
         copy.wait_send()
-    for name in ("y", "z", "xy", "xz", "yz"):
+    for name in ("y", "z", "xr", "xy", "xz", "yz"):
         finish(name)
 
 
@@ -587,6 +676,10 @@
             pltpu.VMEM((2, cx, cz), F32),
             pltpu.VMEM((4 * cx, cz), F32),
             pltpu.VMEM((2, 2, cy, cz), F32),
+            pltpu.VMEM((2, 4, 1, cz), F32),
+            pltpu.VMEM((2, 4, 1, cz), F32),
+            pltpu.VMEM((2, cx, cz), F32),
+            pltpu.VMEM((2 * cx, cz), F32),
             pltpu.VMEM((2, 2, cx, cz), F32),
             pltpu.VMEM((2, 2, cx, cz), F32),
             pltpu.VMEM((2, cx, cz), F32),
@@ -604,8 +697,8 @@
             pltpu.SemaphoreType.DMA((2,)),
             pltpu.SemaphoreType.DMA((2,)),
             pltpu.SemaphoreType.REGULAR((relays,)),
-            pltpu.SemaphoreType.DMA((6,)),
-            pltpu.SemaphoreType.DMA((6,)),
+            pltpu.SemaphoreType.DMA((7,)),
+            pltpu.SemaphoreType.DMA((7,)),
             pltpu.SemaphoreType.DMA((len(stages),)),
             pltpu.SemaphoreType.DMA((len(stages),)),
         ],

time: 20.4 us -> 19.6 us (0.961)
  Pallas kernels: 19 us -> 18.1 us
    pallas_call x1, Pallas kernels: 18 us -> 17.1 us  [per_device(): pl.pallas_call(functools.partial(kernel, sizes, stages, relays), out_shap...]
where the time goes in v6:
time: 19.6 us; the launch traced here: 19.4 us
  Pallas kernels  18.1 us (92%)
  between operations  1.28 us (7%)
    pallas_call x1, Pallas kernels, per_device(): pl.pallas_call(functools.partial(kernel, sizes, stages, relays), out_shap...  17.1 us
    pallas_call x1, Pallas kernels, combined(): pl.pallas_call(combine, out_shape=(box, box), in_specs=[vmem] * 4, out_sp...  0.99 us

profile of v6, /device:TPU:0, one launch (start us, length us, event | category | flops | bytes accessed | tf_op | source)
XLA Modules:
  0.0 19.4 jit_solution(15663732202709888080)
XLA Ops:
  1.3 17.1 %shard_map.77 = (f32[16,64,128]{2,1,0:T(8,128)S(1)}, f32[16,64,128]{2,1,0:T(8,128)S(1)}, f32[16,64,128]{2,1,0:T(8,128)S(1)}, f32[8,128]{1,0:T(8,128)S(1)}) custom-call(s32[6]{0:T(128)} %bitcast.4, s32[6]{0:T(128)} %bitcast.5, s32[1,1,1]{2,1,0:T(1,128)S(6)} %copy.8.live_hbm, f32[6,128,128]{2,1,0:T(8,128)} %bitcast.3, f32[16,64,128]{2,1,0:T(8,128)} %right_hbm.1, ...), custom_call_target="tpu_custom_call" | custom-call | tf_op jit(solution)/shard_map/pallas_call | solution.py:658
  18.4 1.0 %shard_map.78 = (f32[16,64,128]{2,1,0:T(8,128)}, f32[16,64,128]{2,1,0:T(8,128)}) custom-call(f32[16,64,128]{2,1,0:T(8,128)S(1)} %get-tuple-element.6.load_ref, f32[16,64,128]{2,1,0:T(8,128)S(1)} %get-tuple-element.7.p_ref, f32[16,64,128]{2,1,0:T(8,128)S(1)} %get-tuple-element.8.q_ref, f32[8,128]{1,0:T(8,128)S(1)} %get-tuple-element.9.coef_ref), custom_call_target="tpu_custom_call" | custom-call | tf_op jit(solution)/shard_map/pallas_call | solution.py:640

commit v7 on v6

--- a/solution.py
+++ b/solution.py
@@ -43,13 +43,17 @@
     return rounds
 
 
+def message_rows(cx, cy, nx, ny, nz):
+    return (2 * cy + 4) * nx + 2 * cx * ny + cx * nz + nx * ny + nx * nz + 8 * ny * nz
+
+
 def kernel(
     sizes, stages, relays,
     rank_hbm, tile_hbm, live_hbm, face_hbm, right_hbm, diag_hbm,
     load_v, p_v, q_v, coef_ref,
     rank_ref, tile_ref, live_ref, face_v, diag_v, sums_v,
-    send_v, stag_v, recv_v, rtag_v, turned_v, rows_v, drows_v, cols_v,
-    hx_v, xr_v, hxr_v, qrows_v, qcols_v, ysend_v, hy_v, zsend_v, hz_v, xy_v, hxy_v, yz_v, hyz_v, xz_v, hxz_v, mix_v, part_v, gath_v,
+    send_v, scard_v, recv_v, rcard_v, turned_v, rows_v, drows_v, cols_v,
+    hx_v, xr_v, hxr_v, qrows_v, qcols_v, ysend_v, hy_v, zsend_v, hz_v, xy_v, hxy_v, yz_v, hyz_v, xz_v, hxz_v, mix_v, tally_v, part_v, gath_v,
     in_sem, a2a_send, a2a_recv, relay_sem, halo_send, halo_recv, red_send, red_recv,
 ):
     cx, cy, cz = load_v.shape
@@ -122,10 +126,6 @@
     greet(barrier)
 
     messages = {"x": [], "z": [], "y": [], "xr": [], "xy": [], "xz": [], "yz": []}
-    places = {
-        "x": hx_v, "y": hy_v, "z": hz_v, "xr": hxr_v, "xy": hxy_v, "xz": hxz_v, "yz": hyz_v,
-    }
-    kinds = list(messages)
     for s in range(2):
         end = (cx - 1) * s
         messages["x"].append(((("gx", s),), load_v.at[end], lambda s: hx_v.at[s, 0]))
@@ -144,41 +144,44 @@
                 ((("gy", s), ("gz", t)), yz_v, lambda s, t: hyz_v.at[2 * s + t])
             )
 
-    def send(name):
-        for sides, src, place in messages[name]:
-            @pl.when(near_all(sides))
-            def _():
-                pltpu.make_async_remote_copy(
-                    src_ref=src, dst_ref=place(*[1 - side for _, side in sides]),
-                    send_sem=halo_send.at[kinds.index(name)],
-                    recv_sem=halo_recv.at[kinds.index(name)],
-                    device_id={
-                        axis: lax.rem(at[axis] + (1 if side else sizes[axis] - 1), sizes[axis])
-                        for axis, side in sides
-                    },
-                    device_id_type=MESH,
-                ).start()
-
-    def settle(name, act):
-        count = jnp.int32(1)
-        for axis, _ in messages[name][0][0]:
-            count = count * sum(jnp.where(near(axis, side), 1, 0) for side in range(2))
-        for found in (1, 2, 4)[:places[name].shape[0] // 2 + 1]:
-            @pl.when(count == found)
-            def _():
-                slots = places[name].at[pl.ds(0, found)]
-                act(pltpu.make_async_remote_copy(
-                    src_ref=slots, dst_ref=slots,
-                    send_sem=halo_send.at[kinds.index(name)],
-                    recv_sem=halo_recv.at[kinds.index(name)],
-                    device_id=beside({"gx": 1}), device_id_type=MESH,
-                ))
-
-    def receive(name):
-        settle(name, lambda copy: copy.wait_recv())
-
-    def finish(name):
-        settle(name, lambda copy: copy.wait_send())
+    def send(name, part=None):
+        for order, (sides, src, place) in enumerate(messages[name]):
+            if part in (None, order % 2):
+                @pl.when(near_all(sides))
+                def _():
+                    pltpu.make_async_remote_copy(
+                        src_ref=src, dst_ref=place(*[1 - side for _, side in sides]),
+                        send_sem=halo_send.at[0], recv_sem=halo_recv.at[0],
+                        device_id={
+                            axis: lax.rem(
+                                at[axis] + (1 if side else sizes[axis] - 1), sizes[axis]
+                            )
+                            for axis, side in sides
+                        },
+                        device_id_type=MESH,
+                    ).start()
+
+    def settle(act):
+        beside_on = {
+            axis: sum(jnp.where(near(axis, side), 1, 0) for side in range(2)) for axis in AXES
+        }
+        counts = [range(min(1, sizes[axis] - 1), min(2, sizes[axis] - 1) + 1) for axis in AXES]
+        for nx in counts[0]:
+            for ny in counts[1]:
+                for nz in counts[2]:
+                    lines = message_rows(cx, cy, nx, ny, nz)
+                    if lines:
+                        @pl.when(
+                            (beside_on["gx"] == nx) & (beside_on["gy"] == ny)
+                            & (beside_on["gz"] == nz)
+                        )
+                        def _():
+                            span = tally_v.at[pl.ds(0, lines)]
+                            act(pltpu.make_async_remote_copy(
+                                src_ref=span, dst_ref=span,
+                                send_sem=halo_send.at[0], recv_sem=halo_recv.at[0],
+                                device_id=beside({"gx": 1}), device_id_type=MESH,
+                            ))
 
     for name in messages:
         for sides, _, place in messages[name]:
@@ -195,7 +198,6 @@
     row8 = lax.broadcasted_iota(jnp.int32, (8, cz), 0)
     layer = lax.broadcasted_iota(jnp.int32, (cx, cz), 0)
     lane_x = lax.broadcasted_iota(jnp.int32, (cx, cz), 1)
-    right_half = lane >= cz // 2
     ends = (lane == 0) | (lane == cz - 1)
 
     def turn(values, by, axis=1):
@@ -218,7 +220,6 @@
     high = whole.astype(jnp.bfloat16)
     rest = whole - high.astype(F32)
     middle = rest.astype(jnp.bfloat16)
-    low = (rest - middle.astype(F32)).astype(jnp.bfloat16)
     column = lax.broadcasted_iota(jnp.int32, (8, cz), 0)
     column = jnp.where(column < 2, column, cz // 2 - 4 + column)
     choice = (lax.broadcasted_iota(jnp.int32, (8, cz), 1) // 2 == column) & (column < cz // 2)
@@ -229,11 +230,11 @@
             choice, values, (((1,), (1,)), ((), ())), preferred_element_type=F32
         )
 
-    columns = columns_of(low) + columns_of(middle) + columns_of(high)
+    columns = columns_of(middle) + columns_of(high)
     sums_v[...] = (
-        jnp.dot(low, pair, preferred_element_type=F32)
-        + jnp.dot(middle, pair, preferred_element_type=F32)
-    ) + jnp.dot(high, pair, preferred_element_type=F32)
+        jnp.dot(middle, pair, preferred_element_type=F32)
+        + jnp.dot(high, pair, preferred_element_type=F32)
+    )
 
     target = [rank_ref[b] for b in range(blocks)]
     alive = [live_ref[0, 0, 0] > b for b in range(blocks)]
@@ -251,41 +252,49 @@
         even = jnp.where(lane1 < cz // 2, first[0:1], last[1:2])
         other = jnp.where(lane1 < cz // 2, first[3:4], last[2:3])
         edges.append(jnp.where(lax.rem(tile_ref[b], 2) == 0, even, other))
-    for k in range(group):
-        dest = lax.rem(at["gx"] + k, group)
-        outer = [jnp.zeros((1, cz), F32) for _ in range(CAP)]
-        total = jnp.zeros((cy, cz), F32)
-        tags = jnp.full((1, cz), -1.0, F32)
-        for b in range(blocks):
-            code = jnp.where(alive[b] & (target[b] == dest), position[b], CAP)
-            left, right = jnp.where(code == 0, 1.0, 0.0), jnp.where(code == 1, 1.0, 0.0)
-            weight = jnp.where(lane1 < cz // 2, left, right)
-            tag = tile_ref[b].astype(F32)
-            tags = jnp.where(weight > 0.5, tag, tags)
-            values = sums_v[b * cy:(b + 1) * cy]
-            total = total + values * jnp.where(right_half, right, left)
-            outer = [outer[0] + left * edges[b], outer[1] + right * edges[b]]
-        (recv_v if k == 0 else send_v)[k] = total
-        for place, values in enumerate([tags] + outer):
-            (rtag_v if k == 0 else stag_v)[3 * k + place] = values
-
-    pl.semaphore_wait(barrier, greeted())
-    boxes = ((send_v, recv_v), (stag_v, rtag_v))
-
-    def exchange(order, slots, k):
+    cards = []
+    for b in range(blocks):
+        card = jnp.where(row8 < 6, edges[b], (tile_ref[b] + 1).astype(F32))
+        for place, y in enumerate((0, 1, cy - 2, cy - 1)):
+            card = jnp.where(row8 == place, sums_v[b * cy + y:b * cy + y + 1], card)
+        cards.append(card)
+    slot0 = jnp.where(row8 == 4, 1, jnp.where(row8 == 5, 0, jnp.where(lane8 < cz // 2, 1, 0)))
+    slot0 = slot0.astype(F32)
+    slot1 = 1.0 - slot0
+    boxes = ((send_v, recv_v), (scard_v, rcard_v))
+
+    def exchange(order, slots, offset):
         src, dst = boxes[order]
         return pltpu.make_async_remote_copy(
             src_ref=src.at[slots], dst_ref=dst.at[slots],
             send_sem=a2a_send.at[order], recv_sem=a2a_recv.at[order],
-            device_id=beside({"gx": k}), device_id_type=MESH,
+            device_id=across(offset), device_id_type=MESH,
         )
 
-    for k in range(1, group):
-        for order in range(2):
-            exchange(order, pl.ds(k * (1, 3)[order], (1, 3)[order]), k).start()
+    pl.semaphore_wait(barrier, greeted())
+    shares = {}
+    for k in reversed(range(group)):
+        dest = across({"gx": k})["gx"] if k else at["gx"]
+        total = jnp.zeros((8, cz), F32)
+        for b in range(blocks):
+            code = jnp.where(alive[b] & (target[b] == dest), position[b], CAP)
+            left, right = jnp.where(code == 0, 1.0, 0.0), jnp.where(code == 1, 1.0, 0.0)
+            shares[k, b] = left, right
+            total = total + cards[b] * (slot0 * left + slot1 * right)
+        (rcard_v if k == 0 else scard_v)[k] = total
+        if k:
+            exchange(1, pl.ds(k, 1), {"gx": k}).start()
+    for k in reversed(range(group)):
+        total = jnp.zeros((cy, cz), F32)
+        for b in range(blocks):
+            left, right = shares[k, b]
+            values = sums_v[b * cy:(b + 1) * cy]
+            total = total + values * jnp.where(lane1 < cz // 2, left, right)
+        (recv_v if k == 0 else send_v)[k] = total
+        if k:
+            exchange(0, pl.ds(k, 1), {"gx": k}).start()
     arrivals = [
-        exchange(order, pl.ds(step, step * (group - 1)), 1)
-        for order, step in enumerate((1, 3)) if group > 1
+        exchange(order, pl.ds(1, group - 1), {"gx": 1}) for order in (1, 0) if group > 1
     ]
     greet(relay_sem.at[0])
     loads[1].wait()
@@ -311,16 +320,15 @@
         pl.semaphore_wait(relay_sem.at[relay], greeted(min(relay + 1, 2)))
         if relay < relays - 1:
             greet(relay_sem.at[relay + 1], 2)
-    for copy in arrivals:
+    for copy in arrivals[:1]:
         copy.wait_recv()
 
+    received, sources = [], []
     for k in range(group):
-        turned_v[k] = pltpu.roll(recv_v[k], cz // 2, axis=1)
-    sources = []
-    for k in range(group):
-        tags = rtag_v[3 * k]
-        swapped = pltpu.roll(jnp.broadcast_to(tags, (8, cz)), cz // 2, axis=1)[:1]
-        sources += [(recv_v.at[k], tags), (turned_v.at[k], swapped)]
+        card = rcard_v[k]
+        swapped = pltpu.roll(card, cz // 2, axis=1)
+        received += [(card, card[6:7] - 1.0), (swapped, swapped[6:7] - 1.0)]
+        sources += [(recv_v.at[k], received[-2][1]), (turned_v.at[k], received[-1][1])]
     half1 = jnp.where(lane1 >= cz // 2, 1, 0)
 
     def scatter(x):
@@ -344,10 +352,10 @@
 
     want = (2 * layer + jnp.where(lane_x >= cz // 2, 1, 0)).astype(F32)
     faces = [rows_v[place] for place in range(4)]
-    for values, tags in sources:
+    for card, tags in received:
         hit = jnp.broadcast_to(tags, (cx, cz)) == want
-        for place, y in enumerate((0, 1, cy - 2, cy - 1)):
-            spread = jnp.broadcast_to(values[y:y + 1], (cx, cz))
+        for place in range(4):
+            spread = jnp.broadcast_to(card[place:place + 1], (cx, cz))
             faces[place] = faces[place] + jnp.where(hit, spread, 0.0)
     for side in range(2):
         face, second = faces[3 * side], faces[1 + side]
@@ -367,11 +375,11 @@
     own_tile = (2 * (line % cx) + line // cx).astype(F32)
     turned = cols_v[:2 * cx]
     for k in range(group):
-        tags = rtag_v[3 * k]
+        card, tags = received[2 * k]
         for place in range(CAP):
             tag = tags[:, :1] if place == 0 else tags[:, cz - 1:]
             hit = jnp.broadcast_to(tag, (2 * cx, cz)) == own_tile
-            values = jnp.broadcast_to(rtag_v[3 * k + 1 + place], (2 * cx, cz))
+            values = jnp.broadcast_to(card[4 + place:5 + place], (2 * cx, cz))
             turned = turned + jnp.where(hit, values, 0.0)
     around = jnp.where(lane_z == 0, 0.0, turn(turned, 1)) + turn(turned, cz // 2)
     around = around + jnp.where(lane_z == cy - 1, 0.0, turn(turned, -1))
@@ -399,11 +407,19 @@
     for name in ("yz", "xz", "xr"):
         send(name)
 
-    for x in (0, 1, cx - 2, cx - 1):
+    for copy in arrivals[1:]:
+        copy.wait_recv()
+    for k in range(group):
+        turned_v[k] = pltpu.roll(recv_v[k], cz // 2, axis=1)
+
+    for x in (0, cx - 1):
+        scatter(x)
+    send("x", 0)
+    for x in (1, cx - 2):
         scatter(x)
     for x in (0, cx - 1):
         p_v[x] = inside(load_v, x)
-    send("x")
+    send("x", 1)
 
     def fold(acc, values):
         for part in range(cy // 8):
@@ -415,15 +431,18 @@
     for x in range(1, cx - 1):
         p_v[x] = inside(load_v, x)
     acc = [jnp.zeros((8, cz), F32) for _ in range(4)]
+    for x in range(cx):
+        q_v[x] = inside(p_v, x)
+    for x in range(cx):
+        load, p, q = load_v[x], p_v[x], q_v[x]
+        pairs = ((load, load), (load, p), (p, p), (p, q))
+        acc = [fold(total, one * other) for total, (one, other) in zip(acc, pairs)]
     image = jnp.zeros((cy, cz), F32)
     for x in range(cx):
-        load, p, q = load_v[x], p_v[x], inside(p_v, x)
-        q_v[x] = q
-        pairs = ((load, load), (load, p), (p, p), (p, q))
-        acc = [fold(total, one * other) for total, (one, other) in zip(acc, pairs)]
+        q = q_v[x]
         for side in range(2):
             y = (cy - 1) * side
-            qrows_v[side, x:x + 1] = q[y:y + 1]
+            qrows_v[side, x:x + 1] = q_v[x, y:y + 1]
             spot = cx * side + x
             image = jnp.where(lane == spot, turn(q, spot + side), image)
     qcols_v[...] = jnp.concatenate([image, jnp.zeros((cz - cy, cz), F32)], axis=0).T[:2 * cx]
@@ -433,11 +452,29 @@
         bottom = plane[cy - 8:] - jnp.where(row8 == 7, last, 0.0)
         return jnp.concatenate([top, plane[8:cy - 8], bottom], axis=0)
 
-    for name in ("x", "xr", "y", "z", "xy", "xz", "yz"):
-        receive(name)
+    settle(lambda copy: copy.wait_recv())
     there = {
         (axis, side): jnp.where(near(axis, side), 1.0, 0.0) for axis in AXES for side in range(2)
     }
+    def add(at_sum, values):
+        for part in range(values.shape[0] // 8):
+            acc[at_sum] = acc[at_sum] + values[8 * part:8 * part + 8]
+
+    def face_sums(h, halo, load, p, q, stencil):
+        add(1, -(load * h))
+        add(2, h * (h - 2.0 * p))
+        add(3, h * (stencil + halo - 2.0 * q) - p * halo)
+
+    rows = [jnp.zeros((1, cz), F32) for _ in range(4)]
+    for side in range(2):
+        x = (cx - 1) * side
+        h, load = hx_v[side, 0], load_v[x]
+        around = jnp.where(lane == 0, 0.0, turn(h, 1))
+        around = around + jnp.where(lane == cz - 1, 0.0, turn(h, -1))
+        around = around + jnp.where(row == 0, 0.0, turn(h, 1, 0))
+        around = around + jnp.where(row == cy - 1, 0.0, turn(h, -1, 0))
+        halo = hx_v[side, 1] - there["gx", side] * load
+        face_sums(h, halo, load, p_v[x], q_v[x], diag_v[x] * h - around)
     y_halo = []
     for side in range(2):
         halo = hy_v[side, 1] - there["gy", side] * ysend_v[side, 0]
@@ -460,25 +497,6 @@
             parts.append(piece)
         halves.append(jnp.concatenate(parts, axis=0))
 
-    def add(at_sum, values):
-        for part in range(values.shape[0] // 8):
-            acc[at_sum] = acc[at_sum] + values[8 * part:8 * part + 8]
-
-    def face_sums(h, halo, load, p, q, stencil):
-        add(1, -(load * h))
-        add(2, h * (h - 2.0 * p))
-        add(3, h * (stencil + halo - 2.0 * q) - p * halo)
-
-    rows = [jnp.zeros((1, cz), F32) for _ in range(4)]
-    for side in range(2):
-        x = (cx - 1) * side
-        h, load = hx_v[side, 0], load_v[x]
-        around = jnp.where(lane == 0, 0.0, turn(h, 1))
-        around = around + jnp.where(lane == cz - 1, 0.0, turn(h, -1))
-        around = around + jnp.where(row == 0, 0.0, turn(h, 1, 0))
-        around = around + jnp.where(row == cy - 1, 0.0, turn(h, -1, 0))
-        halo = hx_v[side, 1] - there["gx", side] * load
-        face_sums(h, halo, load, p_v[x], q_v[x], diag_v[x] * h - around)
     y_stencil = []
     for side in range(2):
         h = hy_v[side, 0]
@@ -545,7 +563,7 @@
         return jnp.concatenate([columns, jnp.zeros((cz, cz - 2 * cx), F32)], axis=1)
 
     def complete():
-        finish("x")
+        settle(lambda copy: copy.wait_send())
         l_halo = columned([hz_v[0], hz_v[1]])[:cy]
         for x in range(cx):
             plane = p_v[x] - jnp.where(ends, turn(l_halo, -2 * x - 1), 0.0)
@@ -591,35 +609,34 @@
             span = gath_v.at[pl.ds(slot, len(offsets))]
             waiting.append(part(offsets[0], span, span))
             waiting[-1].wait_recv()
-        for place in range(len(offsets)):
-            mine = mine + gath_v[slot + place]
+        parts = [mine] + [gath_v[slot + place] for place in range(len(offsets))]
+        while len(parts) > 1:
+            parts = [sum(parts[n:n + 2]) for n in range(0, len(parts), 2)]
+        mine = parts[0]
         slot += len(offsets)
 
     sums = jnp.sum(jnp.where(own, mine, 0.0), axis=1, keepdims=True)
     s0, s1, s2, s3 = (sums[n:n + 1] for n in range(4))
-    step = 6.0 * s0 + s1
-    a = s0 / step
-    c = s1 / step
-    norm = c * c * s0 - 2.0 * a * c * s1 + a * a * s2
-    e = c + norm / s0
-    curve = 6.0 * (e * e * s0 - 2.0 * e * a * s1 + a * a * s2) + (
-        e * e * s1 - 2.0 * e * a * s2 + a * a * s3
+    inverse = 1.0 / (6.0 * s0 + s1)
+    a, c, m, third = s0 * inverse, s1 * inverse, s2 * inverse, s3 * inverse
+    growth = a * m - c * c
+    e = c + growth
+    curve = 6.0 * (e * e * a - 2.0 * e * a * c + a * a * m) + (
+        e * e * c - 2.0 * e * a * m + a * a * third
     )
-    b = norm / curve
+    b = a * growth / curve
     x_load, x_p = a + b * e, b * a
     r_load, r_p, r_q = c - 6.0 * b * e, a + b * (e - 6.0 * a), b * a
     for order, value in enumerate((x_load, x_p, r_load, r_p, r_q)):
         coef_ref[order:order + 1] = jnp.broadcast_to(value, (1, cz))
     for copy in arrivals + waiting:
         copy.wait_send()
-    for name in ("y", "z", "xr", "xy", "xz", "yz"):
-        finish(name)
 
 
 def combine(load_ref, p_ref, q_ref, coef_ref, x_hbm, r_hbm, x_v, r_v, sem):
     cx = load_ref.shape[0]
     x_load, x_p, r_load, r_p, r_q = (coef_ref[n:n + 1] for n in range(5))
-    pieces = 4
+    pieces = 8
     for piece in range(pieces):
         first, last = cx * piece // pieces, cx * (piece + 1) // pieces
         for x in range(first, last):
@@ -668,9 +685,9 @@
             pltpu.VMEM((cx, cy, cz), F32),
             pltpu.VMEM((blocks * cy, cz), F32),
             pltpu.VMEM((group, cy, cz), F32),
-            pltpu.VMEM((3 * group, 1, cz), F32),
+            pltpu.VMEM((group, 8, cz), F32),
             pltpu.VMEM((group, cy, cz), F32),
-            pltpu.VMEM((3 * group, 1, cz), F32),
+            pltpu.VMEM((group, 8, cz), F32),
             pltpu.VMEM((group, cy, cz), F32),
             pltpu.VMEM((4, cx, cz), F32),
             pltpu.VMEM((2, cx, cz), F32),
@@ -691,14 +708,15 @@
             pltpu.VMEM((4, 1, cz), F32),
             pltpu.VMEM((4, 1, cz), F32),
             pltpu.VMEM((2 * cx, cz), F32),
+            pltpu.VMEM((message_rows(cx, cy, 2, 2, 2), 1, cz), F32),
             pltpu.VMEM((len(stages), 1, cz), F32),
             pltpu.VMEM((slots, 1, cz), F32),
             pltpu.SemaphoreType.DMA((6,)),
             pltpu.SemaphoreType.DMA((2,)),
             pltpu.SemaphoreType.DMA((2,)),
             pltpu.SemaphoreType.REGULAR((relays,)),
-            pltpu.SemaphoreType.DMA((7,)),
-            pltpu.SemaphoreType.DMA((7,)),
+            pltpu.SemaphoreType.DMA((1,)),
+            pltpu.SemaphoreType.DMA((1,)),
             pltpu.SemaphoreType.DMA((len(stages),)),
             pltpu.SemaphoreType.DMA((len(stages),)),
         ],

time: 19.6 us -> 18.7 us (0.954)
  Pallas kernels: 18.1 us -> 17.2 us
    pallas_call x1, Pallas kernels: 17.1 us -> 16.3 us  [per_device(): pl.pallas_call(functools.partial(kernel, sizes, stages, relays), out_shap...]
where the time goes in v7:
time: 18.7 us; the launch traced here: 18.5 us
  Pallas kernels  17.2 us (92%)
  between operations  1.28 us (7%)
    pallas_call x1, Pallas kernels, per_device(): pl.pallas_call(functools.partial(kernel, sizes, stages, relays), out_shap...  16.3 us
    pallas_call x1, Pallas kernels, combined(): pl.pallas_call(combine, out_shape=(box, box), in_specs=[vmem] * 4, out_sp...  0.98 us

profile of v7, /device:TPU:0, one launch (start us, length us, event | category | flops | bytes accessed | tf_op | source)
XLA Modules:
  0.0 18.5 jit_solution(18051927074544308484)
XLA Ops:
  1.3 16.3 %shard_map.77 = (f32[16,64,128]{2,1,0:T(8,128)S(1)}, f32[16,64,128]{2,1,0:T(8,128)S(1)}, f32[16,64,128]{2,1,0:T(8,128)S(1)}, f32[8,128]{1,0:T(8,128)S(1)}) custom-call(s32[6]{0:T(128)} %bitcast.4, s32[6]{0:T(128)} %bitcast.5, s32[1,1,1]{2,1,0:T(1,128)S(6)} %copy.8.live_hbm, f32[6,128,128]{2,1,0:T(8,128)} %bitcast.3, f32[16,64,128]{2,1,0:T(8,128)} %right_hbm.1, ...), custom_call_target="tpu_custom_call" | custom-call | tf_op jit(solution)/shard_map/pallas_call | solution.py:675
  17.5 1.0 %shard_map.78 = (f32[16,64,128]{2,1,0:T(8,128)}, f32[16,64,128]{2,1,0:T(8,128)}) custom-call(f32[16,64,128]{2,1,0:T(8,128)S(1)} %get-tuple-element.6.load_ref, f32[16,64,128]{2,1,0:T(8,128)S(1)} %get-tuple-element.7.p_ref, f32[16,64,128]{2,1,0:T(8,128)S(1)} %get-tuple-element.8.q_ref, f32[8,128]{1,0:T(8,128)S(1)} %get-tuple-element.9.coef_ref), custom_call_target="tpu_custom_call" | custom-call | tf_op jit(solution)/shard_map/pallas_call | solution.py:657

commit v8 on v7

--- a/solution.py
+++ b/solution.py
@@ -35,16 +35,17 @@
 
 
 def relays_of(sizes, stages):
-    rounds = 1
+    rounds = 2
     for axes in stages:
         steps = [sizes[axis] - 1 for axis in axes if axis != "gx"]
         single = sum(n % 2 for n in steps) + (1 if "gx" in axes and sizes["gx"] > 1 else 0)
-        rounds = max(rounds, 1 + sum(n // 2 for n in steps) + max(0, single - 3))
+        rounds = max(rounds, 1 + sum(n // 2 for n in steps) + max(0, single - 2))
     return rounds
 
 
 def message_rows(cx, cy, nx, ny, nz):
-    return (2 * cy + 4) * nx + 2 * cx * ny + cx * nz + nx * ny + nx * nz + 8 * ny * nz
+    rest = 4 * nx + 2 * cx * ny + cx * nz + nx * ny + nx * nz + 8 * ny * nz
+    return 2 * cy * nx, rest
 
 
 def kernel(
@@ -144,6 +145,9 @@
                 ((("gy", s), ("gz", t)), yz_v, lambda s, t: hyz_v.at[2 * s + t])
             )
 
+    def kind_of(name):
+        return 0 if name == "x" else 1
+
     def send(name, part=None):
         for order, (sides, src, place) in enumerate(messages[name]):
             if part in (None, order % 2):
@@ -151,7 +155,8 @@
                 def _():
                     pltpu.make_async_remote_copy(
                         src_ref=src, dst_ref=place(*[1 - side for _, side in sides]),
-                        send_sem=halo_send.at[0], recv_sem=halo_recv.at[0],
+                        send_sem=halo_send.at[kind_of(name)],
+                        recv_sem=halo_recv.at[kind_of(name)],
                         device_id={
                             axis: lax.rem(
                                 at[axis] + (1 if side else sizes[axis] - 1), sizes[axis]
@@ -161,25 +166,25 @@
                         device_id_type=MESH,
                     ).start()
 
-    def settle(act):
+    def settle(kind, act):
         beside_on = {
             axis: sum(jnp.where(near(axis, side), 1, 0) for side in range(2)) for axis in AXES
         }
         counts = [range(min(1, sizes[axis] - 1), min(2, sizes[axis] - 1) + 1) for axis in AXES]
         for nx in counts[0]:
-            for ny in counts[1]:
-                for nz in counts[2]:
-                    lines = message_rows(cx, cy, nx, ny, nz)
+            for ny in counts[1] if kind else (0,):
+                for nz in counts[2] if kind else (0,):
+                    lines = message_rows(cx, cy, nx, ny, nz)[kind]
+                    found = beside_on["gx"] == nx
+                    if kind:
+                        found = found & (beside_on["gy"] == ny) & (beside_on["gz"] == nz)
                     if lines:
-                        @pl.when(
-                            (beside_on["gx"] == nx) & (beside_on["gy"] == ny)
-                            & (beside_on["gz"] == nz)
-                        )
+                        @pl.when(found)
                         def _():
                             span = tally_v.at[pl.ds(0, lines)]
                             act(pltpu.make_async_remote_copy(
                                 src_ref=span, dst_ref=span,
-                                send_sem=halo_send.at[0], recv_sem=halo_recv.at[0],
+                                send_sem=halo_send.at[kind], recv_sem=halo_recv.at[kind],
                                 device_id=beside({"gx": 1}), device_id_type=MESH,
                             ))
 
@@ -316,10 +321,12 @@
             upper = jnp.where(lane == spot, turn(weights, spot + side), upper)
     cols_v[...] = jnp.concatenate([upper, lower], axis=0).T[:4 * cx]
 
-    for relay in range(relays):
+    def hear(relay):
         pl.semaphore_wait(relay_sem.at[relay], greeted(min(relay + 1, 2)))
         if relay < relays - 1:
             greet(relay_sem.at[relay + 1], 2)
+
+    hear(0)
     for copy in arrivals[:1]:
         copy.wait_recv()
 
@@ -420,6 +427,8 @@
     for x in (0, cx - 1):
         p_v[x] = inside(load_v, x)
     send("x", 1)
+    for relay in range(1, relays - 1):
+        hear(relay)
 
     def fold(acc, values):
         for part in range(cy // 8):
@@ -452,7 +461,7 @@
         bottom = plane[cy - 8:] - jnp.where(row8 == 7, last, 0.0)
         return jnp.concatenate([top, plane[8:cy - 8], bottom], axis=0)
 
-    settle(lambda copy: copy.wait_recv())
+    settle(1, lambda copy: copy.wait_recv())
     there = {
         (axis, side): jnp.where(near(axis, side), 1.0, 0.0) for axis in AXES for side in range(2)
     }
@@ -466,15 +475,6 @@
         add(3, h * (stencil + halo - 2.0 * q) - p * halo)
 
     rows = [jnp.zeros((1, cz), F32) for _ in range(4)]
-    for side in range(2):
-        x = (cx - 1) * side
-        h, load = hx_v[side, 0], load_v[x]
-        around = jnp.where(lane == 0, 0.0, turn(h, 1))
-        around = around + jnp.where(lane == cz - 1, 0.0, turn(h, -1))
-        around = around + jnp.where(row == 0, 0.0, turn(h, 1, 0))
-        around = around + jnp.where(row == cy - 1, 0.0, turn(h, -1, 0))
-        halo = hx_v[side, 1] - there["gx", side] * load
-        face_sums(h, halo, load, p_v[x], q_v[x], diag_v[x] * h - around)
     y_halo = []
     for side in range(2):
         halo = hy_v[side, 1] - there["gy", side] * ysend_v[side, 0]
@@ -529,6 +529,27 @@
         return second, third + one * other_halo + other * one_halo
 
     for s in range(2):
+        for t in range(2):
+            goal = (cy - 1) * s
+            spot, spot_in = ((0, 1), (cz - 1, cz - 2))[t]
+            second, third = edge_sums(
+                turn(hy_v[s, 0], goal - spot), turn(hy_v[s, 0], goal - spot_in),
+                turn(y_halo[s], goal - spot), z_h[t], z_halves[t], z_stencil[t],
+            )
+            add(2, jnp.where(lane_x == goal, second, 0.0))
+            add(3, jnp.where(lane_x == goal, third, 0.0))
+
+    settle(0, lambda copy: copy.wait_recv())
+    for side in range(2):
+        x = (cx - 1) * side
+        h, load = hx_v[side, 0], load_v[x]
+        around = jnp.where(lane == 0, 0.0, turn(h, 1))
+        around = around + jnp.where(lane == cz - 1, 0.0, turn(h, -1))
+        around = around + jnp.where(row == 0, 0.0, turn(h, 1, 0))
+        around = around + jnp.where(row == cy - 1, 0.0, turn(h, -1, 0))
+        halo = hx_v[side, 1] - there["gx", side] * load
+        face_sums(h, halo, load, p_v[x], q_v[x], diag_v[x] * h - around)
+    for s in range(2):
         x = (cx - 1) * s
         for t in range(2):
             y, y_in = ((0, 1), (cy - 1, cy - 2))[t]
@@ -547,15 +568,6 @@
             used1 = lane1 < cy
             rows[2] = rows[2] + jnp.where(used1, second, 0.0)
             rows[3] = rows[3] + jnp.where(used1, third, 0.0)
-            goal = (cy - 1) * s
-            spot, spot_in = ((0, 1), (cz - 1, cz - 2))[t]
-            second, third = edge_sums(
-                turn(hy_v[s, 0], goal - spot), turn(hy_v[s, 0], goal - spot_in),
-                turn(y_halo[s], goal - spot), z_h[t], z_halves[t], z_stencil[t],
-            )
-            add(2, jnp.where(lane_x == goal, second, 0.0))
-            add(3, jnp.where(lane_x == goal, third, 0.0))
-
     def columned(halves):
         for side in range(2):
             mix_v[pl.ds(1 - side, cx, stride=2), :] = halves[side]
@@ -563,7 +575,8 @@
         return jnp.concatenate([columns, jnp.zeros((cz, cz - 2 * cx), F32)], axis=1)
 
     def complete():
-        settle(lambda copy: copy.wait_send())
+        for kind in range(2):
+            settle(kind, lambda copy: copy.wait_send())
         l_halo = columned([hz_v[0], hz_v[1]])[:cy]
         for x in range(cx):
             plane = p_v[x] - jnp.where(ends, turn(l_halo, -2 * x - 1), 0.0)
@@ -581,13 +594,15 @@
                     plane = plane - hx_v[side, 1] + there["gx", side] * load_v[x]
             q_v[x] = plane
 
+    own = row8 == lane8 // (cz // 4)
     mine = jnp.zeros((8, cz), F32)
     for order in range(4):
-        mine = jnp.where(row8 == order, jnp.sum(acc[order], axis=0, keepdims=True) + rows[order], mine)
-    mine = mine + pltpu.roll(mine, cz // 2, axis=1)
-    mine = mine + pltpu.roll(mine, cz // 4, axis=1)
-    own = row8 == lane8 // (cz // 4)
-    mine = jnp.sum(jnp.where(own, mine, 0.0), axis=0, keepdims=True)
+        total = acc[order] + jnp.where(row8 == 0, rows[order], 0.0)
+        total = total + pltpu.roll(total, cz // 2, axis=1)
+        total = total + pltpu.roll(total, cz // 4, axis=1)
+        mine = jnp.where(lane8 // (cz // 4) == order, total, mine)
+    mine = jnp.sum(mine, axis=0, keepdims=True)
+    hear(relays - 1)
     slot = 0
     waiting = []
     for order, axes in enumerate(stages):
@@ -636,7 +651,7 @@
 def combine(load_ref, p_ref, q_ref, coef_ref, x_hbm, r_hbm, x_v, r_v, sem):
     cx = load_ref.shape[0]
     x_load, x_p, r_load, r_p, r_q = (coef_ref[n:n + 1] for n in range(5))
-    pieces = 8
+    pieces = 16
     for piece in range(pieces):
         first, last = cx * piece // pieces, cx * (piece + 1) // pieces
         for x in range(first, last):
@@ -708,15 +723,15 @@
             pltpu.VMEM((4, 1, cz), F32),
             pltpu.VMEM((4, 1, cz), F32),
             pltpu.VMEM((2 * cx, cz), F32),
-            pltpu.VMEM((message_rows(cx, cy, 2, 2, 2), 1, cz), F32),
+            pltpu.VMEM((max(message_rows(cx, cy, 2, 2, 2)), 1, cz), F32),
             pltpu.VMEM((len(stages), 1, cz), F32),
             pltpu.VMEM((slots, 1, cz), F32),
             pltpu.SemaphoreType.DMA((6,)),
             pltpu.SemaphoreType.DMA((2,)),
             pltpu.SemaphoreType.DMA((2,)),
             pltpu.SemaphoreType.REGULAR((relays,)),
-            pltpu.SemaphoreType.DMA((1,)),
-            pltpu.SemaphoreType.DMA((1,)),
+            pltpu.SemaphoreType.DMA((2,)),
+            pltpu.SemaphoreType.DMA((2,)),
             pltpu.SemaphoreType.DMA((len(stages),)),
             pltpu.SemaphoreType.DMA((len(stages),)),
         ],

time: 18.7 us -> 18.5 us (0.989)
  no operation moved by 1% of the time
where the time goes in v8:
time: 18.5 us; the launch traced here: 18.4 us
  Pallas kernels  17.1 us (92%)
  between operations  1.28 us (7%)
    pallas_call x1, Pallas kernels, per_device(): pl.pallas_call(functools.partial(kernel, sizes, stages, relays), out_shap...  16.1 us
    pallas_call x1, Pallas kernels, combined(): pl.pallas_call(combine, out_shape=(box, box), in_specs=[vmem] * 4, out_sp...  0.97 us

profile of v8, /device:TPU:0, one launch (start us, length us, event | category | flops | bytes accessed | tf_op | source)
XLA Modules:
  0.0 18.4 jit_solution(1508391078713900196)
XLA Ops:
  1.3 16.1 %shard_map.77 = (f32[16,64,128]{2,1,0:T(8,128)S(1)}, f32[16,64,128]{2,1,0:T(8,128)S(1)}, f32[16,64,128]{2,1,0:T(8,128)S(1)}, f32[8,128]{1,0:T(8,128)S(1)}) custom-call(s32[6]{0:T(128)} %bitcast.4, s32[6]{0:T(128)} %bitcast.5, s32[1,1,1]{2,1,0:T(1,128)S(6)} %copy.8.live_hbm, f32[6,128,128]{2,1,0:T(8,128)} %bitcast.3, f32[16,64,128]{2,1,0:T(8,128)} %right_hbm.1, ...), custom_call_target="tpu_custom_call" | custom-call | tf_op jit(solution)/shard_map/pallas_call | solution.py:690
  17.4 1.0 %shard_map.78 = (f32[16,64,128]{2,1,0:T(8,128)}, f32[16,64,128]{2,1,0:T(8,128)}) custom-call(f32[16,64,128]{2,1,0:T(8,128)S(1)} %get-tuple-element.6.load_ref, f32[16,64,128]{2,1,0:T(8,128)S(1)} %get-tuple-element.7.p_ref, f32[16,64,128]{2,1,0:T(8,128)S(1)} %get-tuple-element.8.q_ref, f32[8,128]{1,0:T(8,128)S(1)} %get-tuple-element.9.coef_ref), custom_call_target="tpu_custom_call" | custom-call | tf_op jit(solution)/shard_map/pallas_call | solution.py:672

commit v9 on v8

--- a/solution.py
+++ b/solution.py
@@ -44,8 +44,9 @@
 
 
 def message_rows(cx, cy, nx, ny, nz):
-    rest = 4 * nx + 2 * cx * ny + cx * nz + nx * ny + nx * nz + 8 * ny * nz
-    return 2 * cy * nx, rest
+    half = cy // 2
+    faces = 4 * nx + 2 * cx * ny + cx * nz
+    return (cy + half) * nx, faces, nx * ny + nx * nz + 8 * ny * nz, half * nx
 
 
 def kernel(
@@ -94,7 +95,7 @@
         pltpu.make_async_copy(rank_hbm, rank_ref, in_sem.at[4]),
         pltpu.make_async_copy(tile_hbm, tile_ref, in_sem.at[5]),
     ]
-    for copy in loads:
+    for copy in loads[:1] + loads[3:]:
         copy.start()
 
     def within(axis, step):
@@ -126,11 +127,19 @@
     barrier = pltpu.get_barrier_semaphore()
     greet(barrier)
 
-    messages = {"x": [], "z": [], "y": [], "xr": [], "xy": [], "xz": [], "yz": []}
+    half = cy // 2
+    messages = {"x": [], "late": [], "z": [], "y": [], "xr": [], "xy": [], "xz": [], "yz": []}
     for s in range(2):
         end = (cx - 1) * s
         messages["x"].append(((("gx", s),), load_v.at[end], lambda s: hx_v.at[s, 0]))
-        messages["x"].append(((("gx", s),), p_v.at[end], lambda s: hx_v.at[s, 1]))
+        messages["x"].append((
+            (("gx", s),), p_v.at[end, pl.ds(half * s, half)],
+            lambda s: hx_v.at[s, 1, pl.ds(half * (1 - s), half)],
+        ))
+        messages["late"].append((
+            (("gx", s),), p_v.at[end, pl.ds(half * (1 - s), half)],
+            lambda s: hx_v.at[s, 1, pl.ds(half * s, half)],
+        ))
         messages["xr"].append(((("gx", s),), xr_v.at[s], lambda s: hxr_v.at[s]))
         messages["y"].append(((("gy", s),), ysend_v.at[s], lambda s: hy_v.at[s]))
         messages["z"].append(((("gz", s),), zsend_v.at[s], lambda s: hz_v.at[s]))
@@ -146,7 +155,7 @@
             )
 
     def kind_of(name):
-        return 0 if name == "x" else 1
+        return {"x": 0, "y": 1, "z": 1, "xr": 1, "late": 3}.get(name, 2)
 
     def send(name, part=None):
         for order, (sides, src, place) in enumerate(messages[name]):
@@ -172,11 +181,11 @@
         }
         counts = [range(min(1, sizes[axis] - 1), min(2, sizes[axis] - 1) + 1) for axis in AXES]
         for nx in counts[0]:
-            for ny in counts[1] if kind else (0,):
-                for nz in counts[2] if kind else (0,):
+            for ny in counts[1] if kind in (1, 2) else (0,):
+                for nz in counts[2] if kind in (1, 2) else (0,):
                     lines = message_rows(cx, cy, nx, ny, nz)[kind]
                     found = beside_on["gx"] == nx
-                    if kind:
+                    if kind in (1, 2):
                         found = found & (beside_on["gy"] == ny) & (beside_on["gz"] == nz)
                     if lines:
                         @pl.when(found)
@@ -210,6 +219,8 @@
         return values if by == 0 else pltpu.roll(values, by, axis=axis)
 
     loads[0].wait()
+    for copy in loads[1:3]:
+        copy.start()
     for copy in loads[3:]:
         copy.wait()
     pair = (
@@ -374,8 +385,6 @@
         ysend_v[side, 1] = drows_v[side] * face - around
         for s in range(2):
             xy_v[2 * s + side] = face[(cx - 1) * s:(cx - 1) * s + 1]
-    send("xy")
-    send("y")
 
     line = lax.broadcasted_iota(jnp.int32, (2 * cx, cz), 0)
     lane_z = lax.broadcasted_iota(jnp.int32, (2 * cx, cz), 1)
@@ -397,7 +406,6 @@
     turned = jnp.where(lane_z < cy, turned, turn(image, cz // 2))
     for side in range(2):
         zsend_v[side] = turned[cx * side:cx * side + cx]
-    send("z")
     groups = cx // 8
     tile = jnp.zeros((8, cz), F32)
     for side in range(2):
@@ -411,7 +419,7 @@
             xr_v[s, 2 * side] = turned[spot:spot + 1]
             xr_v[s, 2 * side + 1] = deeper[spot:spot + 1]
     yz_v[...] = tile
-    for name in ("yz", "xz", "xr"):
+    for name in ("yz", "xz", "xy", "z", "y", "xr"):
         send(name)
 
     for copy in arrivals[1:]:
@@ -427,6 +435,7 @@
     for x in (0, cx - 1):
         p_v[x] = inside(load_v, x)
     send("x", 1)
+    send("late")
     for relay in range(1, relays - 1):
         hear(relay)
 
@@ -475,28 +484,10 @@
         add(3, h * (stencil + halo - 2.0 * q) - p * halo)
 
     rows = [jnp.zeros((1, cz), F32) for _ in range(4)]
-    y_halo = []
-    for side in range(2):
-        halo = hy_v[side, 1] - there["gy", side] * ysend_v[side, 0]
-        halo = halo - jnp.where(layer == 0, 2.0 * hxy_v[side], 0.0)
-        y_halo.append(halo - jnp.where(layer == cx - 1, 2.0 * hxy_v[2 + side], 0.0))
-    halves = []
-    for side in range(2):
-        halo = hz_v[side] - there["gz", side] * turn(zsend_v[side], cz // 2)
-        for s in range(2):
-            corner = turn(jnp.broadcast_to(hxz_v[2 * s + side], (8, cz)), cz // 2)[:1]
-            halo = halo - jnp.where(layer == (cx - 1) * s, 2.0 * corner, 0.0)
-        parts = []
-        for part in range(groups):
-            piece = halo[8 * part:8 * part + 8]
-            for s in range(2):
-                spot = 2 * (groups * (1 - s) + part) + side
-                goal = cy if s == 0 else 2 * cy - 1
-                corner = turn(hyz_v[2 * s + side], goal - spot)
-                piece = piece - jnp.where(lane8 == goal, 2.0 * corner, 0.0)
-            parts.append(piece)
-        halves.append(jnp.concatenate(parts, axis=0))
-
+    y_base = [hy_v[side, 1] - there["gy", side] * ysend_v[side, 0] for side in range(2)]
+    z_base = [
+        hz_v[side] - there["gz", side] * turn(zsend_v[side], cz // 2) for side in range(2)
+    ]
     y_stencil = []
     for side in range(2):
         h = hy_v[side, 0]
@@ -506,13 +497,13 @@
         around = around + jnp.where(layer == cx - 1, 0.0, turn(h, -1, 0))
         y_stencil.append(drows_v[side] * h - around)
         face_sums(
-            h, y_halo[side], ysend_v[side, 0], ysend_v[side, 1], qrows_v[side], y_stencil[side]
+            h, y_base[side], ysend_v[side, 0], ysend_v[side, 1], qrows_v[side], y_stencil[side]
         )
     z_stencil, z_h, z_halves = [], [], []
     used = lane_x < cy
     for side in range(2):
         h = jnp.where(used, hz_v[side], 0.0)
-        halo = jnp.where(used, turn(halves[side], cz // 2), 0.0)
+        halo = jnp.where(used, turn(z_base[side], cz // 2), 0.0)
         around = turn(h, 1) + jnp.where(lane_x == cz - 1, 0.0, turn(h, -1))
         around = around + jnp.where(layer == 0, 0.0, turn(h, 1, 0))
         around = around + jnp.where(layer == cx - 1, 0.0, turn(h, -1, 0))
@@ -534,11 +525,12 @@
             spot, spot_in = ((0, 1), (cz - 1, cz - 2))[t]
             second, third = edge_sums(
                 turn(hy_v[s, 0], goal - spot), turn(hy_v[s, 0], goal - spot_in),
-                turn(y_halo[s], goal - spot), z_h[t], z_halves[t], z_stencil[t],
+                turn(y_base[s], goal - spot), z_h[t], z_halves[t], z_stencil[t],
             )
             add(2, jnp.where(lane_x == goal, second, 0.0))
             add(3, jnp.where(lane_x == goal, third, 0.0))
 
+    share = [jnp.where((lane1 >= half) == (side == 0), 2.0, 0.0) for side in range(2)]
     settle(0, lambda copy: copy.wait_recv())
     for side in range(2):
         x = (cx - 1) * side
@@ -547,27 +539,69 @@
         around = around + jnp.where(lane == cz - 1, 0.0, turn(h, -1))
         around = around + jnp.where(row == 0, 0.0, turn(h, 1, 0))
         around = around + jnp.where(row == cy - 1, 0.0, turn(h, -1, 0))
-        halo = hx_v[side, 1] - there["gx", side] * load
-        face_sums(h, halo, load, p_v[x], q_v[x], diag_v[x] * h - around)
+        face_sums(h, 0.0, load, p_v[x], q_v[x], diag_v[x] * h - around)
+        first = half * (1 - side)
+        halo = hx_v[side, 1, first:first + half] - there["gx", side] * load[first:first + half]
+        add(3, 2.0 * (h[first:first + half] - p_v[x, first:first + half]) * halo)
     for s in range(2):
         x = (cx - 1) * s
         for t in range(2):
             y, y_in = ((0, 1), (cy - 1, cy - 2))[t]
             second, third = edge_sums(
                 hx_v[s, 0, y:y + 1], hx_v[s, 0, y_in:y_in + 1],
-                hx_v[s, 1, y:y + 1] - there["gx", s] * load_v[x, y:y + 1],
-                hy_v[t, 0, x:x + 1], y_halo[t][x:x + 1], y_stencil[t][x:x + 1],
+                2.0 * (hx_v[s, 1, y:y + 1] - there["gx", s] * load_v[x, y:y + 1])
+                if s != t else jnp.zeros((1, cz), F32),
+                hy_v[t, 0, x:x + 1], y_base[t][x:x + 1], y_stencil[t][x:x + 1],
             )
             rows[2], rows[3] = rows[2] + second, rows[3] + third
             second, third = edge_sums(
                 hxr_v[s, 2 * t], hxr_v[s, 2 * t + 1],
-                turn(jnp.broadcast_to(hxr_v[s, 2 * t], (8, cz)), cz // 2)[:1]
-                - there["gx", s] * zsend_v[t, x:x + 1],
+                share[s] * (
+                    turn(jnp.broadcast_to(hxr_v[s, 2 * t], (8, cz)), cz // 2)[:1]
+                    - there["gx", s] * zsend_v[t, x:x + 1]
+                ),
                 z_h[t][x:x + 1], z_halves[t][x:x + 1], z_stencil[t][x:x + 1],
             )
             used1 = lane1 < cy
             rows[2] = rows[2] + jnp.where(used1, second, 0.0)
             rows[3] = rows[3] + jnp.where(used1, third, 0.0)
+    inner_p = [turn(zsend_v[side], cz // 2) - z_h[side] for side in range(2)]
+    xy_p, xz_p, yz_p = {}, {}, {}
+    for s in range(2):
+        x = (cx - 1) * s
+        for t in range(2):
+            y, z, last = (cy - 1) * t, (cz - 1) * t, (cy - 1) * t
+            ends_z = [
+                jnp.broadcast_to(hz_v[side, x:x + 1, last:last + 1], (1, cz)) for side in range(2)
+            ]
+            tips = jnp.where(lane1 == 0, ends_z[0], jnp.where(lane1 == cz - 1, ends_z[1], 0.0))
+            xy_p[s, t] = (
+                ysend_v[t, 1, x:x + 1] - hy_v[t, 0, x:x + 1] - hx_v[s, 0, y:y + 1] - tips
+            )
+            ends_y = [
+                jnp.broadcast_to(hy_v[side, 0, x:x + 1, z:z + 1], (1, cz)) for side in range(2)
+            ]
+            tips = jnp.where(lane1 == 0, ends_y[0], jnp.where(lane1 == cy - 1, ends_y[1], 0.0))
+            xz_p[s, t] = inner_p[t][x:x + 1] - hxr_v[s, 2 * t] - tips
+            goal, y = (cy - 1) * s, (cy - 1) * s
+            values = inner_p[t] - turn(hy_v[s, 0], goal - z)
+            for side in range(2):
+                tip = jnp.broadcast_to(hx_v[side, 0, y:y + 1, z:z + 1], (cx, cz))
+                values = values - jnp.where(layer == (cx - 1) * side, tip, 0.0)
+            yz_p[s, t] = jnp.where(lane_x == goal, values, 0.0)
+    settle(2, lambda copy: copy.wait_recv())
+    groups = cx // 8
+    for s in range(2):
+        for t in range(2):
+            rows[3] = rows[3] + (3.0 if s != t else 1.0) * xy_p[s, t] * hxy_v[2 * s + t]
+            rows[3] = rows[3] + jnp.where(
+                lane1 < cy, (1.0 + share[s]) * xz_p[s, t] * hxz_v[2 * s + t], 0.0
+            )
+            for part in range(groups):
+                spot = 2 * (groups * (1 - s) + part) + t
+                corner = turn(hyz_v[2 * s + t], (cy - 1) * s - spot)
+                acc[3] = acc[3] + 2.0 * yz_p[s, t][8 * part:8 * part + 8] * corner
+
     def columned(halves):
         for side in range(2):
             mix_v[pl.ds(1 - side, cx, stride=2), :] = halves[side]
@@ -575,8 +609,30 @@
         return jnp.concatenate([columns, jnp.zeros((cz, cz - 2 * cx), F32)], axis=1)
 
     def complete():
-        for kind in range(2):
+        settle(3, lambda copy: copy.wait_recv())
+        for kind in range(4):
             settle(kind, lambda copy: copy.wait_send())
+        y_halo = []
+        for side in range(2):
+            halo = hy_v[side, 1] - there["gy", side] * ysend_v[side, 0]
+            halo = halo - jnp.where(layer == 0, 2.0 * hxy_v[side], 0.0)
+            y_halo.append(halo - jnp.where(layer == cx - 1, 2.0 * hxy_v[2 + side], 0.0))
+        halves = []
+        for side in range(2):
+            halo = hz_v[side] - there["gz", side] * turn(zsend_v[side], cz // 2)
+            for s in range(2):
+                corner = turn(jnp.broadcast_to(hxz_v[2 * s + side], (8, cz)), cz // 2)[:1]
+                halo = halo - jnp.where(layer == (cx - 1) * s, 2.0 * corner, 0.0)
+            parts = []
+            for part in range(groups):
+                piece = halo[8 * part:8 * part + 8]
+                for s in range(2):
+                    spot = 2 * (groups * (1 - s) + part) + side
+                    goal = cy if s == 0 else 2 * cy - 1
+                    corner = turn(hyz_v[2 * s + side], goal - spot)
+                    piece = piece - jnp.where(lane8 == goal, 2.0 * corner, 0.0)
+                parts.append(piece)
+            halves.append(jnp.concatenate(parts, axis=0))
         l_halo = columned([hz_v[0], hz_v[1]])[:cy]
         for x in range(cx):
             plane = p_v[x] - jnp.where(ends, turn(l_halo, -2 * x - 1), 0.0)
@@ -730,8 +786,8 @@
             pltpu.SemaphoreType.DMA((2,)),
             pltpu.SemaphoreType.DMA((2,)),
             pltpu.SemaphoreType.REGULAR((relays,)),
-            pltpu.SemaphoreType.DMA((2,)),
-            pltpu.SemaphoreType.DMA((2,)),
+            pltpu.SemaphoreType.DMA((4,)),
+            pltpu.SemaphoreType.DMA((4,)),
             pltpu.SemaphoreType.DMA((len(stages),)),
             pltpu.SemaphoreType.DMA((len(stages),)),
         ],

time: 18.5 us -> 18.5 us (level)
  no operation moved by 1% of the time
where the time goes in v9:
time: 18.5 us; the launch traced here: 18.4 us
  Pallas kernels  17.1 us (92%)
  between operations  1.28 us (7%)
    pallas_call x1, Pallas kernels, per_device(): pl.pallas_call(functools.partial(kernel, sizes, stages, relays), out_shap...  16.1 us
    pallas_call x1, Pallas kernels, combined(): pl.pallas_call(combine, out_shape=(box, box), in_specs=[vmem] * 4, out_sp...  0.97 us

profile of v9, /device:TPU:0, one launch (start us, length us, event | category | flops | bytes accessed | tf_op | source)
XLA Modules:
  0.0 18.4 jit_solution(13180356117139003645)
XLA Ops:
  1.3 16.1 %shard_map.77 = (f32[16,64,128]{2,1,0:T(8,128)S(1)}, f32[16,64,128]{2,1,0:T(8,128)S(1)}, f32[16,64,128]{2,1,0:T(8,128)S(1)}, f32[8,128]{1,0:T(8,128)S(1)}) custom-call(s32[6]{0:T(128)} %bitcast.4, s32[6]{0:T(128)} %bitcast.5, s32[1,1,1]{2,1,0:T(1,128)S(6)} %copy.8.live_hbm, f32[6,128,128]{2,1,0:T(8,128)} %bitcast.3, f32[16,64,128]{2,1,0:T(8,128)} %right_hbm.1, ...), custom_call_target="tpu_custom_call" | custom-call | tf_op jit(solution)/shard_map/pallas_call | solution.py:746
  17.4 1.0 %shard_map.78 = (f32[16,64,128]{2,1,0:T(8,128)}, f32[16,64,128]{2,1,0:T(8,128)}) custom-call(f32[16,64,128]{2,1,0:T(8,128)S(1)} %get-tuple-element.6.load_ref, f32[16,64,128]{2,1,0:T(8,128)S(1)} %get-tuple-element.7.p_ref, f32[16,64,128]{2,1,0:T(8,128)S(1)} %get-tuple-element.8.q_ref, f32[8,128]{1,0:T(8,128)S(1)} %get-tuple-element.9.coef_ref), custom_call_target="tpu_custom_call" | custom-call | tf_op jit(solution)/shard_map/pallas_call | solution.py:728
